TPU v7x, 8 devices: a whole 2x2x1 slice. The times are simulated.
8 devices in a mesh: dp: 2 (over z, y), tp: 4 (over x, core).
Axes of the slice: x: 2, y: 2, z: 1, core: 2. Of those that a mesh axis runs over, the one named last changes fastest.
Arguments:
- tokens: int32 [2, 768], P('dp'), parts along dimension 0
- positions: int32 [2, 768], P('dp'), parts along dimension 0
- embed_table: bfloat16 [262208, 2560], P('tp')
- w_query: bfloat16 [2560, 8, 256], P(None, 'tp')
- w_key: bfloat16 [2560, 4, 256], P(None, 'tp')
- w_value: bfloat16 [2560, 4, 256], P(None, 'tp')
- w_out: bfloat16 [8, 256, 2560], P('tp')
- w_gate: bfloat16 [2560, 10240], P(None, 'tp')
- w_up: bfloat16 [2560, 10240], P(None, 'tp')
- w_down: bfloat16 [10240, 2560], P('tp')
- norm_pre_att: float32 [2560], replicated
- norm_post_att: float32 [2560], replicated
- norm_pre_ffw: float32 [2560], replicated
- norm_post_ffw: float32 [2560], replicated
Outputs:
- output: bfloat16 [2, 768, 2560], P('dp', 'tp'), parts along dimension 0
There are 2 independent parts. A program takes and returns all parts, laid end to end along the dimension named above; an argument that names none is the same for every part.
All inputs are finite; a program needn't handle non-finite values.
Results may differ from a plain program's by a relative error of at most 0.02.
Values are sent between devices in bfloat16 or wider.
A program may use at most 1.5 GiB of HBM per device.

v0:
```python
import jax
import jax.numpy as jnp
from jax import lax
from jax.sharding import PartitionSpec as P

WINDOW = 4096
QUERY_SCALE = 256.0 ** -0.5
SOFT_CAP = 50.0
NORM_EPS = 1e-6
ROPE_BASE = 10000.0


def rms_norm(hidden, norm_scale):
    hidden = hidden.astype(jnp.float32)
    mean_sq = jnp.mean(hidden * hidden, axis=-1, keepdims=True)
    return (hidden * lax.rsqrt(mean_sq + NORM_EPS) * (1.0 + norm_scale)).astype(jnp.bfloat16)


def rope_tables(positions, head_dim):
    half_dim = head_dim // 2
    inv_freq = ROPE_BASE ** (-2.0 * jnp.arange(half_dim, dtype=jnp.float32) / head_dim)
    angles = positions.astype(jnp.float32)[:, :, None] * inv_freq
    return jnp.cos(angles)[:, :, None, :], jnp.sin(angles)[:, :, None, :]


def apply_rope(states, cos_tab, sin_tab):
    half_dim = states.shape[-1] // 2
    lower_half = states[..., :half_dim]
    upper_half = states[..., half_dim:]
    return jnp.concatenate([lower_half * cos_tab - upper_half * sin_tab, upper_half * cos_tab + lower_half * sin_tab], axis=-1)


def local_attention(q_states, k_states, v_states, positions):
    seq_len = q_states.shape[1]
    q_block = min(128, seq_len)
    key_span = min(seq_len, WINDOW + q_block)

    def one_block(block_idx):
        q_start = block_idx * q_block
        k_start = jnp.maximum(q_start + q_block - key_span, 0)
        q_blk = lax.dynamic_slice_in_dim(q_states, q_start, q_block, axis=1)
        k_blk = lax.dynamic_slice_in_dim(k_states, k_start, key_span, axis=1)
        v_blk = lax.dynamic_slice_in_dim(v_states, k_start, key_span, axis=1)
        q_pos = lax.dynamic_slice_in_dim(positions, q_start, q_block, axis=1)
        k_pos = lax.dynamic_slice_in_dim(positions, k_start, key_span, axis=1)
        scores = jnp.einsum("bqkgd,blkd->bkgql", q_blk, k_blk, preferred_element_type=jnp.float32)
        capped = SOFT_CAP * jnp.tanh(scores / SOFT_CAP)
        offset = q_pos[:, :, None] - k_pos[:, None, :]
        keep_mask = (offset >= 0) & (offset < WINDOW)
        capped = jnp.where(keep_mask[:, None, None, :, :], capped, -1e30)
        att_probs = jax.nn.softmax(capped, axis=-1).astype(jnp.bfloat16)
        att_mix = jnp.einsum("bkgql,blkd->bqkgd", att_probs, v_blk, preferred_element_type=jnp.float32)
        return att_mix.astype(jnp.bfloat16)

    blocks = lax.map(one_block, jnp.arange(seq_len // q_block))
    return jnp.moveaxis(blocks, 0, 1).reshape(q_states.shape)


def decoder_layer(embeds, positions, w_query, w_key, w_value, w_out, w_gate, w_up, w_down, norm_pre_att, norm_post_att, norm_pre_ffw, norm_post_ffw):
    n_batch, seq_len = positions.shape
    model_dim = embeds.shape[-1]
    kv_local, head_dim = w_key.shape[1], w_key.shape[2]
    n_group = w_query.shape[1] // kv_local
    attn_in = lax.all_gather(rms_norm(embeds, norm_pre_att), "tp", axis=1, tiled=True)
    cos_tab, sin_tab = rope_tables(positions, head_dim)
    q_proj = jnp.einsum("bsd,dnh->bsnh", attn_in, w_query, preferred_element_type=jnp.float32)
    q_states = (apply_rope(q_proj, cos_tab, sin_tab) * QUERY_SCALE).astype(jnp.bfloat16)
    q_states = q_states.reshape(n_batch, seq_len, kv_local, n_group, head_dim)
    k_proj = jnp.einsum("bsd,dnh->bsnh", attn_in, w_key, preferred_element_type=jnp.float32)
    k_states = apply_rope(k_proj, cos_tab, sin_tab).astype(jnp.bfloat16)
    v_states = jnp.einsum("bsd,dnh->bsnh", attn_in, w_value, preferred_element_type=jnp.float32).astype(jnp.bfloat16)
    att_mix = local_attention(q_states, k_states, v_states, positions)
    w_out_grp = w_out.reshape(kv_local, n_group, head_dim, model_dim)
    att_part = jnp.einsum("bskgh,kghd->bsd", att_mix, w_out_grp, preferred_element_type=jnp.float32).astype(jnp.bfloat16)
    att_proj = lax.psum_scatter(att_part, "tp", scatter_dimension=1, tiled=True)
    resid_one = (embeds.astype(jnp.float32) + rms_norm(att_proj, norm_post_att).astype(jnp.float32)).astype(jnp.bfloat16)
    mlp_in = lax.all_gather(rms_norm(resid_one, norm_pre_ffw), "tp", axis=1, tiled=True)
    gate_pre = jnp.einsum("bsd,df->bsf", mlp_in, w_gate, preferred_element_type=jnp.float32)
    up_proj = jnp.einsum("bsd,df->bsf", mlp_in, w_up, preferred_element_type=jnp.float32)
    ffn_act = (jax.nn.gelu(gate_pre, approximate=True) * up_proj).astype(jnp.bfloat16)
    down_part = jnp.einsum("bsf,fd->bsd", ffn_act, w_down, preferred_element_type=jnp.float32).astype(jnp.bfloat16)
    down_proj = lax.psum_scatter(down_part, "tp", scatter_dimension=1, tiled=True)
    return (resid_one.astype(jnp.float32) + rms_norm(down_proj, norm_post_ffw).astype(jnp.float32)).astype(jnp.bfloat16)


def solution(mesh):
    in_specs = (P("dp", None), P("dp", None), P("tp", None), P(None, "tp", None), P(None, "tp", None), P(None, "tp", None), P("tp", None, None), P(None, "tp"), P(None, "tp"), P("tp", None), P(None), P(None), P(None), P(None))

    def device_step(tokens, positions, embed_block, w_query, w_key, w_value, w_out, w_gate, w_up, w_down, norm_pre_att, norm_post_att, norm_pre_ffw, norm_post_ffw):
        dev_rank = lax.axis_index("tp")
        vocab_local, model_dim = embed_block.shape
        local_ids = tokens - dev_rank * vocab_local
        in_block = (local_ids >= 0) & (local_ids < vocab_local)
        looked = jnp.take(embed_block, jnp.clip(local_ids, 0, vocab_local - 1), axis=0)
        normalizer = jnp.sqrt(jnp.float32(model_dim)).astype(jnp.bfloat16)
        partial_emb = jnp.where(in_block[:, :, None], looked * normalizer, jnp.zeros((), jnp.bfloat16))
        embeds = lax.psum_scatter(partial_emb, "tp", scatter_dimension=1, tiled=True)
        return decoder_layer(embeds, positions, w_query, w_key, w_value, w_out, w_gate, w_up, w_down, norm_pre_att, norm_post_att, norm_pre_ffw, norm_post_ffw)

    return jax.shard_map(device_step, mesh=mesh, in_specs=in_specs, out_specs=P("dp", "tp", None), check_vma=False)
```

profile of v0, /device:TPU:0, one launch (start us, length us, event | category | flops | bytes accessed | tf_op | source)
XLA Modules:
  0.0 362.3 jit_solution(17623585850331529131)
XLA Ops:
  6.5 0.9 and_reduce_fusion
  7.4 11.7 %gather_fusion = bf16[768,2560]{1,0:T(8,128)(2,1)} fusion(bf16[65552,2560]{1,0:T(8,128)(2,1)} %param.18, s32[1024]{0:T(1024)S(1)} %pad_clamp_fusion), kind=kCustom, calls=%fused_computation | custom fusion | bytes 7867392 | tf_op jit(solution)/shard_map/jit(_take)/gather | solution.py:94
  19.1 4.0 %fusion.38 = bf16[1,768,2560]{2,1,0:T(8,128)(2,1)} fusion(bf16[768,2560]{1,0:T(8,128)(2,1)} %gather_fusion, pred[768]{0:T(1024)(128)(4,1)S(1)} %get-tuple-element.73, pred[768]{0:T(1024)(128)(4,1)S(1)} %get-tuple-element.83), kind=kLoop, calls=%fused_computation.49 | loop fusion | flops 5898240 | bytes 7865856 | tf_op jit(solution)/shard_map/jit(_where)/select_n | solution.py:96
  23.2 0.6 copy-done.6
  23.8 83.8 %reduce-scatter.4.cloned.1.call-done = bf16[1,192,2560]{2,1,0:T(8,128)(2,1)} async-done(((bf16[1,768,2560]{2,1,0:T(8,128)(2,1)}), bf16[1,192,2560]{2,1,0:T(8,128)(2,1)}) %reduce-scatter.4.cloned.1.call-update) | async-done | bytes 983056 | tf_op jit(solution)/shard_map/reduce_scatter | solution.py:97
  107.6 1.5 fusion.50
  109.1 2.4 fusion.52
  111.8 2.2 multiply_cosine_fusion.1
  114.1 27.6 %all-gather.3.cloned.1.call-done = bf16[1,768,2560]{2,1,0:T(8,128)(2,1)} async-done(((bf16[1,192,2560]{2,1,0:T(8,128)(2,1)}), bf16[1,768,2560]{2,1,0:T(8,128)(2,1)}) %all-gather.3.cloned.1.call-update) | async-done | bytes 3932176 | tf_op jit(solution)/shard_map/all_gather | solution.py:64
  141.7 3.7 %fusion.66 = f32[1,768,1,256]{1,3,2,0:T(8,128)S(1)} fusion(bf16[2560,1,256]{2,0,1:T(8,128)(2,1)} %param.20, bf16[1,768,2560]{2,1,0:T(8,128)(2,1)} %all-gather.3.cloned.1.call-done), kind=kOutput, calls=%fused_computation.84 | convolution fusion | flops 1006632960 | bytes 6029312 | tf_op jit(solution)/shard_map/bsd,dnh->bsnh/dot_general | solution.py:69
  145.4 1.7 fusion.86
  147.1 0.9 copy.20
  148.0 5.2 %fusion.59 = f32[1,768,2,256]{1,3,2,0:T(8,128)S(1)} fusion(bf16[2560,2,256]{2,1,0:T(2,128)(2,1)} %param.19, bf16[1,768,2560]{2,1,0:T(8,128)(2,1)} %all-gather.3.cloned.1.call-done), kind=kOutput, calls=%fused_computation.81 | convolution fusion | flops 2013265920 | bytes 8126464 | tf_op jit(solution)/shard_map/bsd,dnh->bsnh/dot_general | solution.py:66
  153.6 1.8 copy-done.10
  155.4 0.4 copy-done.11
  155.8 1.9 fusion.76
  157.7 31.1 %while.10 = (s32[]{:T(128)}, bf16[6,1,128,1,2,256]{5,2,0,4,3,1:T(8,128)(2,1)}, s32[6]{0:T(128)S(1)}, s32[1,768]{1,0:T(1,128)S(1)}, bf16[1,768,1,2,256]{1,4,3,2,0...) while((s32[]{:T(128)}, ...), condition=%wide.region_5.6_spmd, body=%wide.region_2.5_spmd.sunk | while | flops 203554304 | bytes 3621043 | solution.py:55
  157.7 0.6 dynamic_slice.29
  159.1 1.4 fusion.111
  160.9 2.0 fusion.113
  162.9 0.6 dynamic_slice.29
  164.3 1.4 fusion.111
  166.0 2.0 fusion.113
  168.0 0.6 dynamic_slice.29
  169.5 1.5 fusion.111
  171.2 2.0 fusion.113
  173.2 0.6 dynamic_slice.29
  174.7 1.5 fusion.111
  176.4 2.0 fusion.113
  178.4 0.6 dynamic_slice.29
  179.8 1.5 fusion.111
  181.6 2.0 fusion.113
  183.6 0.6 dynamic_slice.29
  185.0 1.5 fusion.111
  186.8 2.0 fusion.113
  188.8 5.2 %fusion.25 = bf16[1,768,2560]{2,1,0:T(8,128)(2,1)} fusion(bf16[768,2,256]{2,0,1:T(8,128)(2,1)} %bitcast.122, bf16[2,256,2560]{2,1,0:T(8,128)(2,1)S(1)} %copy-done), kind=kOutput, calls=%fused_computation.36 | convolution fusion | flops 2015232000 | bytes 7340032 | tf_op jit(solution)/shard_map/bskgh,kghd->bsd/dot_general | solution.py:74
  194.1 0.6 copy-done.7
  194.7 36.1 %reduce-scatter.6.cloned.1.call-done = bf16[1,192,2560]{2,1,0:T(8,128)(2,1)} async-done(((bf16[1,768,2560]{2,1,0:T(8,128)(2,1)}), bf16[1,192,2560]{2,1,0:T(8,128)(2,1)}) %reduce-scatter.6.cloned.1.call-update) | async-done | bytes 983056 | tf_op jit(solution)/shard_map/reduce_scatter | solution.py:75
  230.8 1.5 fusion.44
  232.3 1.8 fusion.54
  234.2 1.3 fusion.56
  235.7 29.9 %all-gather.5.cloned.1.call-done = bf16[1,768,2560]{2,1,0:T(8,128)(2,1)} async-done(((bf16[1,192,2560]{2,1,0:T(8,128)(2,1)}), bf16[1,768,2560]{2,1,0:T(8,128)(2,1)}) %all-gather.5.cloned.1.call-update) | async-done | bytes 3932176 | tf_op jit(solution)/shard_map/all_gather | solution.py:77
  265.6 16.4 %fusion.29 = f32[768,2560]{1,0:T(8,128)} fusion(bf16[2560,2560]{1,0:T(8,128)(2,1)} %param.23, bf16[1,768,2560]{2,1,0:T(8,128)(2,1)} %all-gather.5.cloned.1.call-done), kind=kOutput, calls=%fused_computation.39 | convolution fusion | flops 10066329600 | bytes 24903680 | tf_op jit(solution)/shard_map/bsd,df->bsf/dot_general | solution.py:78
  282.0 32.5 %fusion.26 = bf16[1,768,2560]{2,1,0:T(8,128)(2,1)} fusion(bf16[2560,2560]{1,0:T(8,128)(2,1)} %param.25, f32[768,2560]{1,0:T(8,128)} %fusion.29, bf16[2560,2560]{1,0:T(8,128)(2,1)} %param.24, bf16[1,768,2560]{2,1,0:T(8,128)(2,1)} %all-gather.5.cloned.1.call-done), kind=kOutput, calls=%fused_computation.37 | convolution fusion | flops 20154286080 | bytes 41943040 | tf_op jit(solution)/shard_map/bsf,fd->bsd/dot_general | solution.py:81
  314.5 0.7 copy-done.9
  315.2 36.2 %reduce-scatter.8.cloned.1.call-done = bf16[1,192,2560]{2,1,0:T(8,128)(2,1)} async-done(((bf16[1,768,2560]{2,1,0:T(8,128)(2,1)}), bf16[1,192,2560]{2,1,0:T(8,128)(2,1)}) %reduce-scatter.8.cloned.1.call-update) | async-done | bytes 983056 | tf_op jit(solution)/shard_map/reduce_scatter | solution.py:82
  351.4 1.5 fusion.47
  352.9 2.9 fusion.57
  (70 shorter events, 3.8 us)
Async XLA Ops:
  6.5 182.2 %copy-start = (bf16[2,256,2560]{2,1,0:T(8,128)(2,1)S(1)}, bf16[2,256,2560]{2,1,0:T(8,128)(2,1)}, u32[]{:S(2)}) copy-start(bf16[2,256,2560]{2,1,0:T(8,128)(2,1)} %param.22) | copy-start | bytes 7864324
  6.5 101.1 %reduce-scatter.4.cloned.1.call-start = ((), (), s32[]{:S(2)}) async-start(), calls=%async_computation.3 | async-start | bytes 4915200 | tf_op jit(solution)/shard_map/reduce_scatter | solution.py:97
  23.1 0.7 copy-start.6
  23.1 88.7 %copy-start.5 = (s32[1,768]{1,0:T(1,128)S(1)}, s32[1,768]{1,0:T(1,128)}, u32[]{:S(2)}) copy-start(s32[1,768]{1,0:T(1,128)} %param.17) | copy-start | bytes 9220
  23.1 118.6 %all-gather.3.cloned.1.call-start = ((), (), s32[]{:S(2)}) async-start(), calls=%async_computation.4 | async-start | bytes 4915200 | tf_op jit(solution)/shard_map/all_gather | solution.py:64
  111.5 119.3 %reduce-scatter.6.cloned.1.call-start = ((), (), s32[]{:S(2)}) async-start(), calls=%async_computation.5 | async-start | bytes 4915200 | tf_op jit(solution)/shard_map/reduce_scatter | solution.py:75
  148.0 5.3 %copy-start.4 = (f32[768,128]{0,1:T(8,128)S(1)}, f32[768,128]{0,1:T(8,128)}, u32[]{:S(2)}) copy-start(f32[768,128]{0,1:T(8,128)} %get-tuple-element.82) | copy-start | bytes 1179652
  153.3 2.1 copy-start.10
  153.3 2.5 copy-start.11
  194.0 0.7 copy-start.7
  194.0 0.7 copy-start.8
  194.0 38.4 %copy-start.2 = (bf16[1,192,2560]{2,1,0:T(8,128)(2,1)S(1)}, bf16[1,192,2560]{2,1,0:T(8,128)(2,1)}, u32[]{:S(2)}) copy-start(bf16[1,192,2560]{2,1,0:T(8,128)(2,1)} %reduce-scatter.4.cloned.1.call-done) | copy-start | bytes 2949124
  194.0 71.6 %all-gather.5.cloned.1.call-start = ((), (), s32[]{:S(2)}) async-start(), calls=%async_computation.6 | async-start | bytes 4915200 | tf_op jit(solution)/shard_map/all_gather | solution.py:77
  234.2 47.9 %copy-start.3 = (bf16[1,192,2560]{2,1,0:T(8,128)(2,1)}, bf16[1,192,2560]{2,1,0:T(8,128)(2,1)S(1)}, u32[]{:S(2)}) copy-start(bf16[1,192,2560]{2,1,0:T(8,128)(2,1)S(1)} %get-tuple-element.72) | copy-start | bytes 2949124
  235.5 115.9 %reduce-scatter.8.cloned.1.call-start = ((), (), s32[]{:S(2)}) async-start(), calls=%async_computation.7 | async-start | bytes 4915200 | tf_op jit(solution)/shard_map/reduce_scatter | solution.py:82
  314.5 0.7 copy-start.9
  314.5 41.3 %copy-start.1 = (bf16[2,256,2560]{2,1,0:T(8,128)(2,1)S(1)}, bf16[2,256,2560]{2,1,0:T(8,128)(2,1)}, u32[]{:S(2)}) copy-start(bf16[2,256,2560]{2,1,0:T(8,128)(2,1)} %param.22) | copy-start | bytes 7864324
Sparse Core Ops, SparseCore 0:
  23.2 84.3 reduce-scatter.3
  111.7 29.9 all-gather.2
  194.1 36.6 reduce-scatter.5
  235.6 29.9 all-gather.4
  314.7 36.6 reduce-scatter.7
where the time goes:
time: 363 us; the launch traced here: 362 us
  waiting for transfers between devices  214 us (59%)
  matrix products  85.8 us (24%)
  other arithmetic  24.7 us (7%)
  local copies, waits for them, and re-layouts  20.4 us (6%)
  between operations  13.3 us (4%)
  loops' own time  3.97 us (1%)
    reduce_scatter x1, waiting for transfers between devices, device_step(): lax.psum_scatter(partial_emb, 'tp', scatter_dimension=1, tiled=True)  83.8 us
    reduce_scatter x1, waiting for transfers between devices, decoder_layer(): lax.psum_scatter(down_part, 'tp', scatter_dimension=1, tiled=True)  36.2 us
    reduce_scatter x1, waiting for transfers between devices, decoder_layer(): att_proj = lax.psum_scatter(att_part, 'tp', scatter_dimension=1, tiled=True)  36.1 us
    dot_general x1, matrix products, decoder_layer(): jnp.einsum('bsf,fd->bsd', ffn_act, w_down, preferred_element_type=jnp.flo...  32.5 us
    all_gather x1, waiting for transfers between devices, decoder_layer(): lax.all_gather(rms_norm(resid_one, norm_pre_ffw), 'tp', axis=1, tiled=True)  29.9 us
    all_gather x1, waiting for transfers between devices, decoder_layer(): lax.all_gather(rms_norm(embeds, norm_pre_att), 'tp', axis=1, tiled=True)  27.6 us
    dot_general x1, matrix products, decoder_layer(): jnp.einsum('bsd,df->bsf', mlp_in, w_gate, preferred_element_type=jnp.floa...  16.4 us
    dot_general x6, matrix products, one_block(): jnp.einsum('bkgql,blkd->bqkgd', att_probs, v_blk, preferred_element_type=...  12.1 us
  transfers between devices with their start and end apart: 5, of which 5 were waited for; matrix products, arithmetic and copies ran while one was open for 1% of the time, Pallas kernels for 0%

commit v1 on v0

v1 whole, which is shorter than its diff:
```python
import functools

import jax
import jax.numpy as jnp
from jax import lax
from jax.experimental import pallas as pl
from jax.experimental.pallas import tpu as pltpu
from jax.sharding import PartitionSpec as P

WINDOW = 4096
QUERY_SCALE = 256.0 ** -0.5
SOFT_CAP = 50.0
NORM_EPS = 1e-6
ROPE_BASE = 10000.0

N_CHUNK = 6
ROWS = 128
HALF = 64
SUB = 16
N_TILE = 512
MESH = pl.DeviceIdType.MESH
F32 = jnp.float32
BF16 = jnp.bfloat16


def rms(block, gain):
    mean_sq = jnp.mean(block * block, axis=-1, keepdims=True)
    return block * lax.rsqrt(mean_sq + NORM_EPS) * gain


def layer_kernel(
    part_ref, cos_ref, sin_ref, qpos_ref, kpos_ref,
    wq_hbm, wk_hbm, wv_hbm, wo_hbm, wg_hbm, wu_hbm, wd_hbm,
    g1_ref, g2_ref, g3_ref, g4_ref,
    out_ref,
    wq, wk, wv, wo, wg, wu, wd,
    own, sib, res, y_in, norm, k_all, v_all, o_buf, h_buf, pair_out, pair_in, z_in, stage,
    w_sem, own_sem, sib_ss, sib_rs, ex_ss, ex_rs, a_ss, a_rs, yp_ss, yp_rs,
    yx_ss, yx_rs, m_ss, m_rs, zp_ss, zp_rs, zx_ss, zx_rs, out_ss, out_rs,
):
    dp = lax.axis_index("dp")
    tp = lax.axis_index("tp")
    chip = lax.div(tp, 2)
    core = lax.rem(tp, 2)
    mate = 2 * chip + 1 - core
    far = 2 * (1 - chip) + core

    def remote(src, dst, send_sem, recv_sem, target):
        return pltpu.make_async_remote_copy(
            src_ref=src, dst_ref=dst, send_sem=send_sem, recv_sem=recv_sem,
            device_id=(dp, target), device_id_type=MESH)

    def half_rows(t):
        return pl.ds(pl.multiple_of(t * HALF, HALF), HALF)

    mine = pl.ds(pl.multiple_of(core * HALF, HALF), HALF)
    theirs = pl.ds(pl.multiple_of((1 - core) * HALF, HALF), HALF)

    def own_copy(t):
        rows = pl.ds(pl.multiple_of(t * ROWS + core * HALF, HALF), HALF)
        return pltpu.make_async_copy(part_ref.at[rows], own.at[half_rows(t)], own_sem.at[t])

    def sib_copy(t):
        rows = pl.ds(pl.multiple_of(t * ROWS + (1 - core) * HALF, HALF), HALF)
        return remote(part_ref.at[rows], sib.at[half_rows(t)], sib_ss.at[t], sib_rs.at[t], mate)

    def ex_copy(t):
        return remote(own.at[half_rows(t)], res.at[half_rows(t)], ex_ss.at[t], ex_rs.at[t], far)

    def norm_copy(slot, send_sem, recv_sem):
        return remote(norm.at[slot, mine], norm.at[slot, mine], send_sem, recv_sem, mate)

    def yp_copy():
        return remote(pair_out, pair_in.at[0], yp_ss, yp_rs, mate)

    def yx_copy(t):
        return remote(sib.at[half_rows(t)], y_in.at[half_rows(t)], yx_ss.at[t], yx_rs.at[t], far)

    def m_copy(t):
        slot = lax.rem(t, 2)
        return norm_copy(slot, m_ss.at[slot], m_rs.at[slot])

    def zp_copy(t):
        slot = lax.rem(t, 2)
        return remote(pair_out, pair_in.at[slot], zp_ss, zp_rs.at[slot], mate)

    def zx_copy(t):
        j = lax.rem(t, 3)
        return remote(own.at[half_rows(t)], z_in.at[half_rows(j)], zx_ss.at[j], zx_rs.at[j], far)

    weights = [
        pltpu.make_async_copy(src, dst, w_sem.at[i])
        for i, (src, dst) in enumerate(
            [(wq_hbm, wq), (wk_hbm, wk), (wv_hbm, wv), (wo_hbm, wo), (wg_hbm, wg), (wu_hbm, wu), (wd_hbm, wd)])
    ]

    barrier = pltpu.get_barrier_semaphore()
    for peer in (mate, far):
        pl.semaphore_signal(barrier, inc=1, device_id=(dp, peer), device_id_type=MESH)
    pl.semaphore_wait(barrier, 2)

    for t in range(N_CHUNK):
        sib_copy(t).start()
        own_copy(t).start()
    for copy in weights:
        copy.start()

    def sub_rows(base, i):
        return pl.ds(pl.multiple_of(base + i * SUB, SUB), SUB)

    def combine(dst, other, dst_base, other_base):
        def step(i, carry):
            rows = sub_rows(dst_base, i)
            total = dst[rows, :].astype(F32) + other[sub_rows(other_base, i), :].astype(F32)
            dst[rows, :] = total.astype(BF16)
            return carry
        lax.fori_loop(0, HALF // SUB, step, 0)

    def send_embed(t, carry):
        own_copy(t).wait()
        sib_copy(t).wait_recv()
        combine(own, sib, t * HALF, t * HALF)
        ex_copy(t).start()
        return carry
    lax.fori_loop(0, N_CHUNK, send_embed, 0)

    k_all[...] = jnp.zeros_like(k_all)
    v_all[...] = jnp.zeros_like(v_all)
    gain1 = 1.0 + g1_ref[...]
    gain2 = 1.0 + g2_ref[...]
    gain3 = 1.0 + g3_ref[...]
    gain4 = 1.0 + g4_ref[...]
    for t in range(N_CHUNK):
        sib_copy(t).wait_send()
    for copy in weights[:4]:
        copy.wait()

    def rope(states, cos_tab, sin_tab):
        lower, upper = states[:, :128], states[:, 128:]
        return lower * cos_tab - upper * sin_tab, upper * cos_tab + lower * sin_tab

    def attention_chunk(t, carry):
        base = t * HALF
        ex_copy(t).wait_recv()

        def embed_step(i, c):
            rows = sub_rows(base, i)
            embed = own[rows, :].astype(F32) + res[rows, :].astype(F32)
            res[rows, :] = embed.astype(BF16)
            norm[0, sub_rows(core * HALF, i), :] = rms(embed, gain1).astype(BF16)
            return c
        lax.fori_loop(0, HALF // SUB, embed_step, 0)

        copy = norm_copy(0, a_ss, a_rs)
        copy.start()
        copy.wait()
        act = norm[0]
        rows = pl.ds(pl.multiple_of(t * ROWS, ROWS), ROWS)
        cos_tab, sin_tab = cos_ref[rows, :], sin_ref[rows, :]
        lower, upper = rope(jnp.dot(act, wk[...], preferred_element_type=F32), cos_tab, sin_tab)
        k_all[rows, :128] = lower.astype(BF16)
        k_all[rows, 128:] = upper.astype(BF16)
        v_all[rows, :] = jnp.dot(act, wv[...], preferred_element_type=F32).astype(BF16)
        offset = qpos_ref[rows, :1] - kpos_ref[...]
        keep = (offset >= 0) & (offset < WINDOW)
        for head in range(2):
            proj = jnp.dot(act, wq[:, head * 256:(head + 1) * 256], preferred_element_type=F32)
            lower, upper = rope(proj, cos_tab, sin_tab)
            query = jnp.concatenate([(lower * QUERY_SCALE).astype(BF16), (upper * QUERY_SCALE).astype(BF16)], axis=-1)
            scores = lax.dot_general(query, k_all[...], (((1,), (1,)), ((), ())), preferred_element_type=F32)
            weight = jnp.where(keep, jnp.exp(SOFT_CAP * jnp.tanh(scores * (1.0 / SOFT_CAP))), 0.0)
            weight = weight * (1.0 / jnp.sum(weight, axis=-1, keepdims=True))
            mixed = jnp.dot(weight.astype(BF16), v_all[...], preferred_element_type=F32)
            o_buf[:, head * 256:(head + 1) * 256] = mixed.astype(BF16)

        def out_tile(n, c):
            cols = pl.ds(pl.multiple_of(n * N_TILE, N_TILE), N_TILE)
            sib[half_rows(t), cols] = jnp.dot(o_buf[mine, :], wo[:, cols], preferred_element_type=F32).astype(BF16)
            pair_out[:, cols] = jnp.dot(o_buf[theirs, :], wo[:, cols], preferred_element_type=F32).astype(BF16)
            return c
        lax.fori_loop(0, 2560 // N_TILE, out_tile, 0)
        copy = yp_copy()
        copy.start()
        copy.wait()
        combine(sib, pair_in.at[0], base, 0)
        yx_copy(t).start()
        return carry
    lax.fori_loop(0, N_CHUNK, attention_chunk, 0)

    for t in range(N_CHUNK):
        ex_copy(t).wait_send()
    for copy in weights[4:]:
        copy.wait()

    def mlp_in(t):
        base = t * HALF
        slot = lax.rem(t, 2)
        yx_copy(t).wait_recv()

        def step(i, c):
            rows = sub_rows(base, i)
            proj = (sib[rows, :].astype(F32) + y_in[rows, :].astype(F32)).astype(BF16).astype(F32)
            resid = (res[rows, :].astype(F32) + rms(proj, gain2).astype(BF16).astype(F32)).astype(BF16)
            res[rows, :] = resid
            norm[slot, sub_rows(core * HALF, i), :] = rms(resid.astype(F32), gain3).astype(BF16)
            return c
        lax.fori_loop(0, HALF // SUB, step, 0)
        m_copy(t).start()

    def finish_pair(t):
        zp_copy(t).wait_recv()
        combine(own, pair_in.at[lax.rem(t, 2)], t * HALF, 0)

        @pl.when(lax.div(t, 3) != chip)
        def _():
            zx_copy(t).start()

    mlp_in(0)

    def mlp_chunk(t, carry):
        slot = lax.rem(t, 2)
        m_copy(t).wait()

        def gate_tile(n, c):
            cols = pl.ds(pl.multiple_of(n * N_TILE, N_TILE), N_TILE)
            gate = jnp.dot(norm[slot], wg[:, cols], preferred_element_type=F32)
            up = jnp.dot(norm[slot], wu[:, cols], preferred_element_type=F32)
            h_buf[:, cols] = (jax.nn.gelu(gate, approximate=True) * up).astype(BF16)
            return c
        lax.fori_loop(0, 2560 // N_TILE, gate_tile, 0)

        @pl.when(t > 0)
        def _():
            finish_pair(t - 1)

        @pl.when(t < N_CHUNK - 1)
        def _():
            mlp_in(t + 1)

        @pl.when(t > 0)
        def _():
            zp_copy(t - 1).wait_send()

        def down_tile(n, c):
            cols = pl.ds(pl.multiple_of(n * N_TILE, N_TILE), N_TILE)
            own[half_rows(t), cols] = jnp.dot(h_buf[mine, :], wd[:, cols], preferred_element_type=F32).astype(BF16)
            pair_out[:, cols] = jnp.dot(h_buf[theirs, :], wd[:, cols], preferred_element_type=F32).astype(BF16)
            return c
        lax.fori_loop(0, 2560 // N_TILE, down_tile, 0)
        zp_copy(t).start()
        return carry
    lax.fori_loop(0, N_CHUNK, mlp_chunk, 0)
    finish_pair(N_CHUNK - 1)

    def result(j, dst, dst_base):
        t = 3 * chip + j
        zx_copy(j).wait_recv()

        def step(i, c):
            rows = sub_rows(t * HALF, i)
            proj = (own[rows, :].astype(F32) + z_in[sub_rows(j * HALF, i), :].astype(F32)).astype(BF16).astype(F32)
            final = res[rows, :].astype(F32) + rms(proj, gain4).astype(BF16).astype(F32)
            dst[sub_rows(dst_base, i), :] = final.astype(BF16)
            return c
        lax.fori_loop(0, HALF // SUB, step, 0)

    handover = remote(stage, out_ref.at[pl.ds(HALF, HALF)], out_ss, out_rs, mate)

    @pl.when(core == 0)
    def _():
        result(0, out_ref, 0)
        result(1, out_ref, 2 * HALF)
        result(2, stage, 0)
        handover.start()

    @pl.when(core == 1)
    def _():
        result(0, stage, 0)
        handover.start()
        result(1, out_ref, 0)
        result(2, out_ref, 2 * HALF)

    handover.wait()
    zp_copy(N_CHUNK - 1).wait_send()
    for t in range(N_CHUNK):
        yx_copy(t).wait_send()
    for j in range(3):
        zx_copy(3 * (1 - chip) + j).wait_send()


def run_layer(partial, cos_tab, sin_tab, q_pos, k_pos, w_query, w_key, w_value, w_out, w_gate, w_up, w_down, g1, g2, g3, g4):
    seq, dim = partial.shape
    vmem = pl.BlockSpec(memory_space=pltpu.VMEM)
    hbm = pl.BlockSpec(memory_space=pl.ANY)
    half_all = pltpu.VMEM((seq // 2, dim), BF16)
    dma = pltpu.SemaphoreType.DMA
    return pl.pallas_call(
        layer_kernel,
        name="layer",
        out_shape=jax.ShapeDtypeStruct((seq // 4, dim), BF16),
        in_specs=[hbm] + [vmem] * 4 + [hbm] * 7 + [vmem] * 4,
        out_specs=vmem,
        scratch_shapes=[
            pltpu.VMEM(w_query.shape, BF16), pltpu.VMEM(w_key.shape, BF16), pltpu.VMEM(w_value.shape, BF16),
            pltpu.VMEM(w_out.shape, BF16), pltpu.VMEM(w_gate.shape, BF16), pltpu.VMEM(w_up.shape, BF16),
            pltpu.VMEM(w_down.shape, BF16),
            half_all, half_all, half_all, half_all,
            pltpu.VMEM((2, ROWS, dim), BF16),
            pltpu.VMEM((seq, 256), BF16), pltpu.VMEM((seq, 256), BF16),
            pltpu.VMEM((ROWS, 512), BF16), pltpu.VMEM((ROWS, dim), BF16),
            pltpu.VMEM((HALF, dim), BF16), pltpu.VMEM((2, HALF, dim), BF16),
            pltpu.VMEM((3 * HALF, dim), BF16), pltpu.VMEM((HALF, dim), BF16),
            dma((7,)), dma((N_CHUNK,)), dma((N_CHUNK,)), dma((N_CHUNK,)), dma((N_CHUNK,)), dma((N_CHUNK,)),
            dma, dma, dma, dma,
            dma((N_CHUNK,)), dma((N_CHUNK,)), dma((2,)), dma((2,)), dma, dma((2,)),
            dma((3,)), dma((3,)), dma, dma,
        ],
        compiler_params=pltpu.CompilerParams(
            collective_id=0, has_side_effects=True, vmem_limit_bytes=67043328),
    )(partial, cos_tab, sin_tab, q_pos, k_pos, w_query, w_key, w_value, w_out, w_gate, w_up, w_down, g1, g2, g3, g4)


def solution(mesh):
    in_specs = (P("dp", None), P("dp", None), P("tp", None), P(None, "tp", None), P(None, "tp", None), P(None, "tp", None), P("tp", None, None), P(None, "tp"), P(None, "tp"), P("tp", None), P(None), P(None), P(None), P(None))

    def device_step(tokens, positions, embed_block, w_query, w_key, w_value, w_out, w_gate, w_up, w_down, g1, g2, g3, g4):
        dev_rank = lax.axis_index("tp")
        vocab_local, model_dim = embed_block.shape
        tokens, positions = tokens[0], positions[0]
        seq = tokens.shape[0]
        local_ids = tokens - dev_rank * vocab_local
        in_block = (local_ids >= 0) & (local_ids < vocab_local)
        looked = jnp.take(embed_block, jnp.clip(local_ids, 0, vocab_local - 1), axis=0)
        normalizer = jnp.sqrt(jnp.float32(model_dim)).astype(BF16)
        partial = jnp.where(in_block[:, None], looked * normalizer, jnp.zeros((), BF16))
        inv_freq = ROPE_BASE ** (-2.0 * jnp.arange(128, dtype=F32) / 256)
        angles = positions.astype(F32)[:, None] * inv_freq
        q_pos = jnp.broadcast_to(positions[:, None], (seq, 128))
        row = lambda gain: gain.reshape(1, model_dim)
        out = run_layer(
            partial, jnp.cos(angles), jnp.sin(angles), q_pos, positions.reshape(1, seq),
            w_query.reshape(model_dim, 512), w_key.reshape(model_dim, 256), w_value.reshape(model_dim, 256),
            w_out.reshape(512, model_dim), w_gate, w_up, w_down, row(g1), row(g2), row(g3), row(g4))
        return out[None]

    return jax.shard_map(device_step, mesh=mesh, in_specs=in_specs, out_specs=P("dp", "tp", None), check_vma=False)
```

time: 363 us -> 214 us (0.59)
  waiting for transfers between devices: 214 us -> 0 us
  Pallas kernels: 0 us -> 179 us
  matrix products: 85.8 us -> 0 us
  other arithmetic: 24.7 us -> 9.26 us
  between operations: 13.3 us -> 0.05 us
  loops' own time: 3.97 us -> 0 us
    pallas_call x0 -> x1, Pallas kernels: none -> 179 us  [run_layer(): pl.pallas_call(layer_kernel, name='layer', out_shape=jax.ShapeDtypeStruct...]
    reduce_scatter x3 -> x0, waiting for transfers between devices: 156 us -> none  [the longest x1 83.8 us: device_step(): lax.psum_scatter(partial_emb, 'tp', scatter_dimension=1, tiled=True)]
    dot_general x18 -> x0, matrix products: 85.8 us -> none  [the longest x1 32.5 us: decoder_layer(): jnp.einsum('bsf,fd->bsd', ffn_act, w_down, preferred_element_type=jnp.flo...]
    all_gather x2 -> x0, waiting for transfers between devices: 57.5 us -> none  [the longest x1 29.9 us: decoder_layer(): lax.all_gather(rms_norm(resid_one, norm_pre_ffw), 'tp', axis=1, tiled=True)]
    reduce_sum x10 -> x0, other arithmetic: 7.91 us -> none  [the longest x4 6.26 us: rms_norm(): mean_sq = jnp.mean(hidden * hidden, axis=-1, keepdims=True)]
    convert_element_type x5 -> x1, other arithmetic: 6.75 us -> 0.01 us  [device_step(): angles = positions.astype(F32)[:, None] * inv_freq]
    reshape x0 -> x4, local copies, waits for them, and re-layouts: none -> 5.24 us  [device_step(): row = lambda gain: gain.reshape(1, model_dim)]
    another operation x1 -> x0, loops' own time: 3.97 us -> none  [local_attention(): blocks = lax.map(one_block, jnp.arange(seq_len // q_block))]
  transfers between devices with their start and end apart: 5 -> 0, of which waited for: 5 -> 0; matrix products, arithmetic and copies ran while one was open for 1% -> 0% of each run, Pallas kernels for 0% -> 0%
where the time goes in v1:
time: 214 us; the launch traced here: 212 us
  Pallas kernels  179 us (84%)
  local copies, waits for them, and re-layouts  23.7 us (11%)
  other arithmetic  9.26 us (4%)
    pallas_call x1, Pallas kernels, run_layer(): pl.pallas_call(layer_kernel, name='layer', out_shape=jax.ShapeDtypeStruct...  179 us
    gather x1, local copies, waits for them, and re-layouts, device_step(): jnp.take(embed_block, jnp.clip(local_ids, 0, vocab_local - 1), axis=0)  11.6 us
    unnamed x2, local copies, waits for them, and re-layouts  5.9 us
    reshape x4, local copies, waits for them, and re-layouts, device_step(): row = lambda gain: gain.reshape(1, model_dim)  5.24 us

profile of v1, /device:TPU:0, one launch (start us, length us, event | category | flops | bytes accessed | tf_op | source)
XLA Modules:
  0.0 211.8 jit_solution(11016433413230813514)
XLA Ops:
  0.0 0.7 and_reduce_fusion
  0.7 0.7 reduce.3
  1.4 0.7 fusion
  2.2 0.7 clamp_reduce_fusion
  2.9 1.3 reshape.88.g1_ref
  4.2 1.3 reshape.89.g2_ref
  5.5 1.3 reshape.90.g3_ref
  6.8 1.3 reshape.91.g4_ref
  8.1 0.9 broadcast_in_dim.37.qpos_ref
  9.0 2.5 %multiply_sine_fusion = (f32[768,128]{1,0:T(8,128)}, f32[768,128]{1,0:T(8,128)}) fusion(f32[128]{0:T(128)S(1)} %multiply_power_fusion, f32[768]{0:T(1024)S(1)} %convert_element_type.7), kind=kLoop, calls=%fused_computation.2 | loop fusion | flops 98304 | bytes 790016 | tf_op jit(solution)/shard_map/sin | solution.py:341
  11.5 3.7 %copy.15 = bf16[320,8,2,256]{3,1,2,0:T(8,128)(2,1)} copy(bf16[320,8,2,256]{3,2,1,0:T(2,128)(2,1)} %bitcast.11) | data formatting | bytes 5242880
  15.2 11.6 %gather_fusion = bf16[768,2560]{1,0:T(8,128)(2,1)} fusion(bf16[65552,2560]{1,0:T(8,128)(2,1)} %param.16, s32[1024]{0:T(1024)S(1)} %pad_clamp_fusion), kind=kCustom, calls=%fused_computation | custom fusion | bytes 7867392 | tf_op jit(solution)/shard_map/jit(_take)/gather | solution.py:333
  26.8 4.0 %multiply_select_fusion.part_ref = bf16[768,2560]{1,0:T(8,128)(2,1)} fusion(bf16[768,2560]{1,0:T(8,128)(2,1)} %gather_fusion, pred[768]{0:T(1024)(128)(4,1)S(1)} %compare_and_fusion, pred[768]{0:T(1024)(128)(4,1)S(1)} %and_reduce_fusion), kind=kLoop, calls=%fused_computation.1 | loop fusion | flops 5898240 | bytes 7865856 | tf_op jit(solution)/shard_map/jit(_where)/select_n | solution.py:335
  30.8 178.8 %layer.1 = bf16[192,2560]{1,0:T(8,128)(2,1)} custom-call(bf16[768,2560]{1,0:T(8,128)(2,1)} %multiply_select_fusion.part_ref, f32[768,128]{1,0:T(8,128)} %get-tuple-element.6.cos_ref, f32[768,128]{1,0:T(8,128)} %get-tuple-element.5.sin_ref, s32[768,128]{1,0:T(8,128)} %broadcast_in_dim.37.qpos_ref, s32[1,768]{1,0:T(1,128)} %kpos_ref.1, ...), custom_call_target="tpu_custom_call" | custom-call | tf_op jit(solution)/shard_map/layer/pallas_call | solution.py:297
  209.6 2.2 %copy.17 = bf16[1,192,2560]{2,1,0:T(8,128)(2,1)} copy(bf16[1,192,2560]{2,1,0:T(8,128)(2,1)} %bitcast.9) | data formatting | bytes 1966080
  (4 shorter events, 0.0 us)

commit v2 on v1

--- a/solution.py
+++ b/solution.py
@@ -18,6 +18,9 @@
 HALF = 64
 SUB = 16
 N_TILE = 512
+LEAD = 3
+LAG = 2
+LATE = 4
 MESH = pl.DeviceIdType.MESH
 F32 = jnp.float32
 BF16 = jnp.bfloat16
@@ -29,12 +32,12 @@
 
 
 def layer_kernel(
-    part_ref, cos_ref, sin_ref, qpos_ref, kpos_ref,
+    part_ref, cos_ref, sin_ref, kpos_ref,
     wq_hbm, wk_hbm, wv_hbm, wo_hbm, wg_hbm, wu_hbm, wd_hbm,
     g1_ref, g2_ref, g3_ref, g4_ref,
     out_ref,
     wq, wk, wv, wo, wg, wu, wd,
-    own, sib, res, y_in, norm, k_all, v_all, o_buf, h_buf, pair_out, pair_in, z_in, stage,
+    own, sib, res, y_in, norm, k_all, v_all, o_buf, h_buf, y_out, y_pair, pair_out, pair_in, z_in, stage,
     w_sem, own_sem, sib_ss, sib_rs, ex_ss, ex_rs, a_ss, a_rs, yp_ss, yp_rs,
     yx_ss, yx_rs, m_ss, m_rs, zp_ss, zp_rs, zx_ss, zx_rs, out_ss, out_rs,
 ):
@@ -54,7 +57,6 @@
         return pl.ds(pl.multiple_of(t * HALF, HALF), HALF)
 
     mine = pl.ds(pl.multiple_of(core * HALF, HALF), HALF)
-    theirs = pl.ds(pl.multiple_of((1 - core) * HALF, HALF), HALF)
 
     def own_copy(t):
         rows = pl.ds(pl.multiple_of(t * ROWS + core * HALF, HALF), HALF)
@@ -71,7 +73,7 @@
         return remote(norm.at[slot, mine], norm.at[slot, mine], send_sem, recv_sem, mate)
 
     def yp_copy():
-        return remote(pair_out, pair_in.at[0], yp_ss, yp_rs, mate)
+        return remote(y_out, y_pair, yp_ss, yp_rs, mate)
 
     def yx_copy(t):
         return remote(sib.at[half_rows(t)], y_in.at[half_rows(t)], yx_ss.at[t], yx_rs.at[t], far)
@@ -120,16 +122,16 @@
         own_copy(t).wait()
         sib_copy(t).wait_recv()
         combine(own, sib, t * HALF, t * HALF)
-        ex_copy(t).start()
+
+        @pl.when(t < LEAD)
+        def _():
+            ex_copy(t).start()
         return carry
     lax.fori_loop(0, N_CHUNK, send_embed, 0)
 
     k_all[...] = jnp.zeros_like(k_all)
     v_all[...] = jnp.zeros_like(v_all)
-    gain1 = 1.0 + g1_ref[...]
-    gain2 = 1.0 + g2_ref[...]
-    gain3 = 1.0 + g3_ref[...]
-    gain4 = 1.0 + g4_ref[...]
+    gain1, gain2, gain3, gain4 = [(1.0 + g[...]).reshape(1, -1) for g in (g1_ref, g2_ref, g3_ref, g4_ref)]
     for t in range(N_CHUNK):
         sib_copy(t).wait_send()
     for copy in weights[:4]:
@@ -139,7 +141,11 @@
         lower, upper = states[:, :128], states[:, 128:]
         return lower * cos_tab - upper * sin_tab, upper * cos_tab + lower * sin_tab
 
-    def attention_chunk(t, carry):
+    def split_halves(both):
+        top, bottom = both[:HALF], both[HALF:]
+        return jnp.where(core == 0, top, bottom), jnp.where(core == 0, bottom, top)
+
+    def attention_chunk(t):
         base = t * HALF
         ex_copy(t).wait_recv()
 
@@ -147,21 +153,22 @@
             rows = sub_rows(base, i)
             embed = own[rows, :].astype(F32) + res[rows, :].astype(F32)
             res[rows, :] = embed.astype(BF16)
-            norm[0, sub_rows(core * HALF, i), :] = rms(embed, gain1).astype(BF16)
+            norm[2, sub_rows(core * HALF, i), :] = rms(embed, gain1).astype(BF16)
             return c
         lax.fori_loop(0, HALF // SUB, embed_step, 0)
 
-        copy = norm_copy(0, a_ss, a_rs)
+        copy = norm_copy(2, a_ss, a_rs)
         copy.start()
         copy.wait()
-        act = norm[0]
+        act = norm[2]
         rows = pl.ds(pl.multiple_of(t * ROWS, ROWS), ROWS)
         cos_tab, sin_tab = cos_ref[rows, :], sin_ref[rows, :]
         lower, upper = rope(jnp.dot(act, wk[...], preferred_element_type=F32), cos_tab, sin_tab)
         k_all[rows, :128] = lower.astype(BF16)
         k_all[rows, 128:] = upper.astype(BF16)
         v_all[rows, :] = jnp.dot(act, wv[...], preferred_element_type=F32).astype(BF16)
-        offset = qpos_ref[rows, :1] - kpos_ref[...]
+        q_pos = jnp.broadcast_to(kpos_ref[:, rows], (8, ROWS)).T[:, :1]
+        offset = q_pos - kpos_ref[...]
         keep = (offset >= 0) & (offset < WINDOW)
         for head in range(2):
             proj = jnp.dot(act, wq[:, head * 256:(head + 1) * 256], preferred_element_type=F32)
@@ -175,22 +182,19 @@
 
         def out_tile(n, c):
             cols = pl.ds(pl.multiple_of(n * N_TILE, N_TILE), N_TILE)
-            sib[half_rows(t), cols] = jnp.dot(o_buf[mine, :], wo[:, cols], preferred_element_type=F32).astype(BF16)
-            pair_out[:, cols] = jnp.dot(o_buf[theirs, :], wo[:, cols], preferred_element_type=F32).astype(BF16)
-            return c
-        lax.fori_loop(0, 2560 // N_TILE, out_tile, 0)
+            both = jnp.dot(o_buf[...], wo[:, cols], preferred_element_type=F32).astype(BF16)
+            sib[half_rows(t), cols], y_out[:, cols] = split_halves(both)
+            return c
+        lax.fori_loop(0, 2560 // N_TILE, out_tile, 0, unroll=True)
         copy = yp_copy()
         copy.start()
         copy.wait()
-        combine(sib, pair_in.at[0], base, 0)
+        combine(sib, y_pair, base, 0)
         yx_copy(t).start()
-        return carry
-    lax.fori_loop(0, N_CHUNK, attention_chunk, 0)
-
-    for t in range(N_CHUNK):
-        ex_copy(t).wait_send()
-    for copy in weights[4:]:
-        copy.wait()
+
+        @pl.when(t + LEAD < N_CHUNK)
+        def _():
+            ex_copy(t + LEAD).start()
 
     def mlp_in(t):
         base = t * HALF
@@ -215,10 +219,18 @@
         def _():
             zx_copy(t).start()
 
-    mlp_in(0)
-
-    def mlp_chunk(t, carry):
+    def mlp_chunk(t):
         slot = lax.rem(t, 2)
+
+        @pl.when(t < LATE)
+        def _():
+            mlp_in(t)
+
+        @pl.when(t == 0)
+        def _():
+            for copy in weights[4:]:
+                copy.wait()
+        ex_copy(t).wait_send()
         m_copy(t).wait()
 
         def gate_tile(n, c):
@@ -227,13 +239,13 @@
             up = jnp.dot(norm[slot], wu[:, cols], preferred_element_type=F32)
             h_buf[:, cols] = (jax.nn.gelu(gate, approximate=True) * up).astype(BF16)
             return c
-        lax.fori_loop(0, 2560 // N_TILE, gate_tile, 0)
+        lax.fori_loop(0, 2560 // N_TILE, gate_tile, 0, unroll=True)
 
         @pl.when(t > 0)
         def _():
             finish_pair(t - 1)
 
-        @pl.when(t < N_CHUNK - 1)
+        @pl.when((t + 1 >= LATE) & (t < N_CHUNK - 1))
         def _():
             mlp_in(t + 1)
 
@@ -243,13 +255,22 @@
 
         def down_tile(n, c):
             cols = pl.ds(pl.multiple_of(n * N_TILE, N_TILE), N_TILE)
-            own[half_rows(t), cols] = jnp.dot(h_buf[mine, :], wd[:, cols], preferred_element_type=F32).astype(BF16)
-            pair_out[:, cols] = jnp.dot(h_buf[theirs, :], wd[:, cols], preferred_element_type=F32).astype(BF16)
-            return c
-        lax.fori_loop(0, 2560 // N_TILE, down_tile, 0)
+            both = jnp.dot(h_buf[...], wd[:, cols], preferred_element_type=F32).astype(BF16)
+            own[half_rows(t), cols], pair_out[:, cols] = split_halves(both)
+            return c
+        lax.fori_loop(0, 2560 // N_TILE, down_tile, 0, unroll=True)
         zp_copy(t).start()
+
+    def step(s, carry):
+        @pl.when(s < N_CHUNK)
+        def _():
+            attention_chunk(s)
+
+        @pl.when(s >= LAG)
+        def _():
+            mlp_chunk(s - LAG)
         return carry
-    lax.fori_loop(0, N_CHUNK, mlp_chunk, 0)
+    lax.fori_loop(0, N_CHUNK + LAG, step, 0)
     finish_pair(N_CHUNK - 1)
 
     def result(j, dst, dst_base):
@@ -288,7 +309,7 @@
         zx_copy(3 * (1 - chip) + j).wait_send()
 
 
-def run_layer(partial, cos_tab, sin_tab, q_pos, k_pos, w_query, w_key, w_value, w_out, w_gate, w_up, w_down, g1, g2, g3, g4):
+def run_layer(partial, cos_tab, sin_tab, k_pos, w_query, w_key, w_value, w_out, w_gate, w_up, w_down, g1, g2, g3, g4):
     seq, dim = partial.shape
     vmem = pl.BlockSpec(memory_space=pltpu.VMEM)
     hbm = pl.BlockSpec(memory_space=pl.ANY)
@@ -298,16 +319,17 @@
         layer_kernel,
         name="layer",
         out_shape=jax.ShapeDtypeStruct((seq // 4, dim), BF16),
-        in_specs=[hbm] + [vmem] * 4 + [hbm] * 7 + [vmem] * 4,
+        in_specs=[hbm] + [vmem] * 3 + [hbm] * 7 + [vmem] * 4,
         out_specs=vmem,
         scratch_shapes=[
             pltpu.VMEM(w_query.shape, BF16), pltpu.VMEM(w_key.shape, BF16), pltpu.VMEM(w_value.shape, BF16),
             pltpu.VMEM(w_out.shape, BF16), pltpu.VMEM(w_gate.shape, BF16), pltpu.VMEM(w_up.shape, BF16),
             pltpu.VMEM(w_down.shape, BF16),
             half_all, half_all, half_all, half_all,
-            pltpu.VMEM((2, ROWS, dim), BF16),
+            pltpu.VMEM((3, ROWS, dim), BF16),
             pltpu.VMEM((seq, 256), BF16), pltpu.VMEM((seq, 256), BF16),
             pltpu.VMEM((ROWS, 512), BF16), pltpu.VMEM((ROWS, dim), BF16),
+            pltpu.VMEM((HALF, dim), BF16), pltpu.VMEM((HALF, dim), BF16),
             pltpu.VMEM((HALF, dim), BF16), pltpu.VMEM((2, HALF, dim), BF16),
             pltpu.VMEM((3 * HALF, dim), BF16), pltpu.VMEM((HALF, dim), BF16),
             dma((7,)), dma((N_CHUNK,)), dma((N_CHUNK,)), dma((N_CHUNK,)), dma((N_CHUNK,)), dma((N_CHUNK,)),
@@ -317,7 +339,7 @@
         ],
         compiler_params=pltpu.CompilerParams(
             collective_id=0, has_side_effects=True, vmem_limit_bytes=67043328),
-    )(partial, cos_tab, sin_tab, q_pos, k_pos, w_query, w_key, w_value, w_out, w_gate, w_up, w_down, g1, g2, g3, g4)
+    )(partial, cos_tab, sin_tab, k_pos, w_query, w_key, w_value, w_out, w_gate, w_up, w_down, g1, g2, g3, g4)
 
 
 def solution(mesh):
@@ -330,17 +352,15 @@
         seq = tokens.shape[0]
         local_ids = tokens - dev_rank * vocab_local
         in_block = (local_ids >= 0) & (local_ids < vocab_local)
-        looked = jnp.take(embed_block, jnp.clip(local_ids, 0, vocab_local - 1), axis=0)
+        looked = embed_block.at[lax.rem(tokens, vocab_local)].get(mode='promise_in_bounds')
         normalizer = jnp.sqrt(jnp.float32(model_dim)).astype(BF16)
         partial = jnp.where(in_block[:, None], looked * normalizer, jnp.zeros((), BF16))
         inv_freq = ROPE_BASE ** (-2.0 * jnp.arange(128, dtype=F32) / 256)
         angles = positions.astype(F32)[:, None] * inv_freq
-        q_pos = jnp.broadcast_to(positions[:, None], (seq, 128))
-        row = lambda gain: gain.reshape(1, model_dim)
         out = run_layer(
-            partial, jnp.cos(angles), jnp.sin(angles), q_pos, positions.reshape(1, seq),
+            partial, jnp.cos(angles), jnp.sin(angles), positions.reshape(1, seq),
             w_query.reshape(model_dim, 512), w_key.reshape(model_dim, 256), w_value.reshape(model_dim, 256),
-            w_out.reshape(512, model_dim), w_gate, w_up, w_down, row(g1), row(g2), row(g3), row(g4))
+            w_out.reshape(512, model_dim), w_gate, w_up, w_down, g1, g2, g3, g4)
         return out[None]
 
     return jax.shard_map(device_step, mesh=mesh, in_specs=in_specs, out_specs=P("dp", "tp", None), check_vma=False)

time: 214 us -> 156 us (0.73)
  Pallas kernels: 179 us -> 128 us
  local copies, waits for them, and re-layouts: 23.7 us -> 16.4 us
    pallas_call x1, Pallas kernels: 179 us -> 128 us  [run_layer(): pl.pallas_call(layer_kernel, name='layer', out_shape=jax.ShapeDtypeStruct...]
    reshape x4 -> x0, local copies, waits for them, and re-layouts: 5.24 us -> none  [device_step(): row = lambda gain: gain.reshape(1, model_dim)]
where the time goes in v2:
time: 156 us; the launch traced here: 154 us
  Pallas kernels  128 us (82%)
  local copies, waits for them, and re-layouts  16.4 us (11%)
  other arithmetic  9.1 us (6%)
    pallas_call x1, Pallas kernels, run_layer(): pl.pallas_call(layer_kernel, name='layer', out_shape=jax.ShapeDtypeStruct...  128 us
    gather x1, local copies, waits for them, and re-layouts, device_step(): embed_block.at[lax.rem(tokens, vocab_local)].get(mode='promise_in_bounds')  10.5 us
    unnamed x2, local copies, waits for them, and re-layouts  5.9 us
    select_n x1, other arithmetic, device_step(): jnp.where(in_block[:, None], looked * normalizer, jnp.zeros((), BF16))  4.48 us

profile of v2, /device:TPU:0, one launch (start us, length us, event | category | flops | bytes accessed | tf_op | source)
XLA Modules:
  0.0 153.9 jit_solution(6781568695811427087)
XLA Ops:
  0.0 0.7 and_reduce_fusion
  0.7 0.7 fusion
  1.4 0.7 convert_reduce_fusion
  2.1 2.5 %multiply_sine_fusion = (f32[768,128]{1,0:T(8,128)}, f32[768,128]{1,0:T(8,128)}) fusion(f32[128]{0:T(128)S(1)} %multiply_power_fusion, f32[768]{0:T(1024)S(1)} %convert_reduce_fusion), kind=kLoop, calls=%fused_computation.2 | loop fusion | flops 98304 | bytes 790016 | tf_op jit(solution)/shard_map/sin | solution.py:361
  4.6 3.7 %copy.15 = bf16[320,8,2,256]{3,1,2,0:T(8,128)(2,1)} copy(bf16[320,8,2,256]{3,2,1,0:T(2,128)(2,1)} %bitcast.11) | data formatting | bytes 5242880
  8.3 10.5 %gather_fusion = bf16[768,2560]{1,0:T(8,128)(2,1)} fusion(bf16[65552,2560]{1,0:T(8,128)(2,1)} %param.16, s32[1024]{0:T(1024)S(1)} %pad_clamp_fusion), kind=kCustom, calls=%fused_computation | custom fusion | bytes 7867392 | tf_op jit(solution)/shard_map/gather | solution.py:355
  18.8 4.5 %multiply_select_fusion.part_ref = bf16[768,2560]{1,0:T(8,128)(2,1)} fusion(bf16[768,2560]{1,0:T(8,128)(2,1)} %gather_fusion, pred[768]{0:T(1024)(128)(4,1)S(1)} %and_reduce_fusion), kind=kLoop, calls=%fused_computation.1 | loop fusion | flops 3932160 | bytes 7865088 | tf_op jit(solution)/shard_map/jit(_where)/select_n | solution.py:357
  23.3 128.4 %layer.1 = bf16[192,2560]{1,0:T(8,128)(2,1)} custom-call(bf16[768,2560]{1,0:T(8,128)(2,1)} %multiply_select_fusion.part_ref, f32[768,128]{1,0:T(8,128)} %get-tuple-element.6.cos_ref, f32[768,128]{1,0:T(8,128)} %get-tuple-element.5.sin_ref, s32[1,768]{1,0:T(1,128)} %kpos_ref.1, bf16[2560,512]{1,0:T(8,128)(2,1)} %bitcast.8, bf16[2560,256]{1,0:T(8,128)(2,1)} %bitcast.12, ...), custom_call_target="tpu_custom_call" | custom-call | tf_op jit(solution)/shard_map/layer/pallas_call | solution.py:318
  151.7 2.2 %copy.17 = bf16[1,192,2560]{2,1,0:T(8,128)(2,1)} copy(bf16[1,192,2560]{2,1,0:T(8,128)(2,1)} %bitcast.9) | data formatting | bytes 1966080
  (2 shorter events, 0.0 us)

commit v3 on v2

--- a/solution.py
+++ b/solution.py
@@ -2,6 +2,7 @@
 
 import jax
 import jax.numpy as jnp
+import numpy as np
 from jax import lax
 from jax.experimental import pallas as pl
 from jax.experimental.pallas import tpu as pltpu
@@ -18,6 +19,7 @@
 HALF = 64
 SUB = 16
 N_TILE = 512
+WQ_ROWS = 320
 LEAD = 3
 LAG = 2
 LATE = 4
@@ -31,14 +33,80 @@
     return block * lax.rsqrt(mean_sq + NORM_EPS) * gain
 
 
+def gather_kernel(scale, ids_ref, id_row_ref, table_ref, part_ref, groups, looked, in_sem, out_sem):
+    block_rows = table_ref.shape[0]
+    first = lax.axis_index("tp") * block_rows
+    spread = 2 ** (block_rows.bit_length() - 1) - 1
+
+    def start_block(b, carry):
+        def start_eight(i, c):
+            for u in range(8):
+                place = b * ROWS + i * 8 + u
+                token = ids_ref[0, place]
+                local = token - first
+                inside = (local >= 0) & (local < block_rows)
+                row = jnp.where(inside, local, token & spread)
+                group = pl.multiple_of(lax.shift_left(lax.shift_right_logical(row, 3), 3), 8)
+                pltpu.make_async_copy(
+                    table_ref.at[pl.ds(group, 8)], groups.at[pl.ds(pl.multiple_of(place * 8, 8), 8)], in_sem.at[b]).start()
+            return c
+        lax.fori_loop(0, ROWS // 8, start_eight, 0)
+        return carry
+    lax.fori_loop(0, N_CHUNK, start_block, 0)
+
+    def out_copy(b):
+        rows = pl.ds(pl.multiple_of(b * ROWS, ROWS), ROWS)
+        return pltpu.make_async_copy(looked.at[rows], part_ref.at[rows], out_sem.at[b])
+
+    def finish_block(b, carry):
+        rows = pl.ds(pl.multiple_of(b * ROWS, ROWS), ROWS)
+        fetched = pl.ds(pl.multiple_of(b * ROWS * 8, ROWS * 8), ROWS * 8)
+        pltpu.make_async_copy(table_ref.at[pl.ds(0, ROWS * 8)], groups.at[fetched], in_sem.at[b]).wait()
+        local = jnp.broadcast_to(id_row_ref[:, rows], (8, ROWS)).T[:, :1] - first
+        inside = (local >= 0) & (local < block_rows)
+        for h in range(2):
+            half = slice(h * HALF, (h + 1) * HALF)
+            place = lax.broadcasted_iota(jnp.int32, (HALF, 1), 0) * 8 + (local[half] & 7)
+            target = jnp.where(inside[half], place, -1)
+            pick = jnp.where(lax.broadcasted_iota(jnp.int32, (HALF, HALF * 8), 1) == target, 1.0, 0.0).astype(BF16)
+            source = pl.ds(pl.multiple_of(b * ROWS * 8 + h * HALF * 8, HALF * 8), HALF * 8)
+            dest = pl.ds(pl.multiple_of(b * ROWS + h * HALF, HALF), HALF)
+            for n in range(2560 // N_TILE):
+                cols = slice(n * N_TILE, (n + 1) * N_TILE)
+                picked = jnp.dot(pick, groups[source, cols], preferred_element_type=F32)
+                looked[dest, cols] = (picked * scale).astype(BF16)
+        out_copy(b).start()
+        return carry
+    lax.fori_loop(0, N_CHUNK, finish_block, 0)
+    for b in range(N_CHUNK):
+        out_copy(b).wait()
+
+
+def gather_rows(tokens, table):
+    seq, dim = tokens.shape[1], table.shape[1]
+    scale = float(np.sqrt(np.float32(dim)).astype(jnp.bfloat16))
+    return pl.pallas_call(
+        functools.partial(gather_kernel, scale),
+        name="gather",
+        out_shape=jax.ShapeDtypeStruct((seq, dim), BF16),
+        in_specs=[pl.BlockSpec(memory_space=pltpu.SMEM), pl.BlockSpec(memory_space=pltpu.VMEM), pl.BlockSpec(memory_space=pl.ANY)],
+        out_specs=pl.BlockSpec(memory_space=pl.ANY),
+        scratch_shapes=[
+            pltpu.VMEM((seq * 8, dim), BF16), pltpu.VMEM((seq, dim), BF16),
+            pltpu.SemaphoreType.DMA((N_CHUNK,)), pltpu.SemaphoreType.DMA((N_CHUNK,)),
+        ],
+        compiler_params=pltpu.CompilerParams(vmem_limit_bytes=56 * 2 ** 20),
+    )(tokens, tokens, table)
+
+
 def layer_kernel(
-    part_ref, cos_ref, sin_ref, kpos_ref,
+    part_ref, kpos_ref, freq_ref,
     wq_hbm, wk_hbm, wv_hbm, wo_hbm, wg_hbm, wu_hbm, wd_hbm,
     g1_ref, g2_ref, g3_ref, g4_ref,
     out_ref,
     wq, wk, wv, wo, wg, wu, wd,
-    own, sib, res, y_in, norm, k_all, v_all, o_buf, h_buf, y_out, y_pair, pair_out, pair_in, z_in, stage,
-    w_sem, own_sem, sib_ss, sib_rs, ex_ss, ex_rs, a_ss, a_rs, yp_ss, yp_rs,
+    wq_in, cos_tabs, sin_tabs, own, sib, res, y_in, norm, k_all, v_all, o_buf, h_buf, y_out, y_pair, pair_out, pair_in, z_in, stage,
+    wq_sem, w_sem, own_sem, sib_ss, sib_rs, ex_ss, ex_rs, a_ss, a_rs, yp_ss, yp_rs,
     yx_ss, yx_rs, m_ss, m_rs, zp_ss, zp_rs, zx_ss, zx_rs, out_ss, out_rs,
 ):
     dp = lax.axis_index("dp")
@@ -93,7 +161,7 @@
     weights = [
         pltpu.make_async_copy(src, dst, w_sem.at[i])
         for i, (src, dst) in enumerate(
-            [(wq_hbm, wq), (wk_hbm, wk), (wv_hbm, wv), (wo_hbm, wo), (wg_hbm, wg), (wu_hbm, wu), (wd_hbm, wd)])
+            [(wk_hbm, wk), (wv_hbm, wv), (wo_hbm, wo), (wg_hbm, wg), (wu_hbm, wu), (wd_hbm, wd)])
     ]
 
     barrier = pltpu.get_barrier_semaphore()
@@ -104,6 +172,14 @@
     for t in range(N_CHUNK):
         sib_copy(t).start()
         own_copy(t).start()
+
+    def wq_copy(i):
+        slot = lax.rem(i, 2)
+        rows = pl.ds(pl.multiple_of(i * WQ_ROWS, WQ_ROWS), WQ_ROWS)
+        return pltpu.make_async_copy(wq_hbm.at[rows], wq_in.at[slot], wq_sem.at[slot])
+
+    wq_copy(0).start()
+    wq_copy(1).start()
     for copy in weights:
         copy.start()
 
@@ -132,9 +208,34 @@
     k_all[...] = jnp.zeros_like(k_all)
     v_all[...] = jnp.zeros_like(v_all)
     gain1, gain2, gain3, gain4 = [(1.0 + g[...]).reshape(1, -1) for g in (g1_ref, g2_ref, g3_ref, g4_ref)]
+
+    def chunk_positions(rows):
+        return jnp.broadcast_to(kpos_ref[:, rows], (8, ROWS)).T[:, :1]
+
+    def tables(t, carry):
+        rows = pl.ds(pl.multiple_of(t * ROWS, ROWS), ROWS)
+        angles = chunk_positions(rows).astype(F32) * freq_ref[...]
+        cos_tabs[rows, :] = jnp.cos(angles)
+        sin_tabs[rows, :] = jnp.sin(angles)
+        return carry
+    lax.fori_loop(0, N_CHUNK, tables, 0)
+
+    def spread_wq(i, carry):
+        slot = lax.rem(i, 2)
+        wq_copy(i).wait()
+        for r in range(0, WQ_ROWS, 64):
+            rows = pl.ds(pl.multiple_of(i * WQ_ROWS + r, 64), 64)
+            for head in range(2):
+                wq[rows, head * 256:(head + 1) * 256] = wq_in[slot, r:r + 64, head, :]
+
+        @pl.when(i + 2 < 2560 // WQ_ROWS)
+        def _():
+            wq_copy(i + 2).start()
+        return carry
+    lax.fori_loop(0, 2560 // WQ_ROWS, spread_wq, 0)
     for t in range(N_CHUNK):
         sib_copy(t).wait_send()
-    for copy in weights[:4]:
+    for copy in weights[:3]:
         copy.wait()
 
     def rope(states, cos_tab, sin_tab):
@@ -162,13 +263,12 @@
         copy.wait()
         act = norm[2]
         rows = pl.ds(pl.multiple_of(t * ROWS, ROWS), ROWS)
-        cos_tab, sin_tab = cos_ref[rows, :], sin_ref[rows, :]
+        cos_tab, sin_tab = cos_tabs[rows, :], sin_tabs[rows, :]
         lower, upper = rope(jnp.dot(act, wk[...], preferred_element_type=F32), cos_tab, sin_tab)
         k_all[rows, :128] = lower.astype(BF16)
         k_all[rows, 128:] = upper.astype(BF16)
         v_all[rows, :] = jnp.dot(act, wv[...], preferred_element_type=F32).astype(BF16)
-        q_pos = jnp.broadcast_to(kpos_ref[:, rows], (8, ROWS)).T[:, :1]
-        offset = q_pos - kpos_ref[...]
+        offset = chunk_positions(rows) - kpos_ref[...]
         keep = (offset >= 0) & (offset < WINDOW)
         for head in range(2):
             proj = jnp.dot(act, wq[:, head * 256:(head + 1) * 256], preferred_element_type=F32)
@@ -215,7 +315,7 @@
         zp_copy(t).wait_recv()
         combine(own, pair_in.at[lax.rem(t, 2)], t * HALF, 0)
 
-        @pl.when(lax.div(t, 3) != chip)
+        @pl.when((lax.div(t, 3) != chip) & (t >= LAG))
         def _():
             zx_copy(t).start()
 
@@ -228,7 +328,7 @@
 
         @pl.when(t == 0)
         def _():
-            for copy in weights[4:]:
+            for copy in weights[3:]:
                 copy.wait()
         ex_copy(t).wait_send()
         m_copy(t).wait()
@@ -265,6 +365,11 @@
         @pl.when(s < N_CHUNK)
         def _():
             attention_chunk(s)
+
+        @pl.when((s == N_CHUNK - 1) & (chip != 0))
+        def _():
+            for t in range(LAG):
+                zx_copy(t).start()
 
         @pl.when(s >= LAG)
         def _():
@@ -309,7 +414,7 @@
         zx_copy(3 * (1 - chip) + j).wait_send()
 
 
-def run_layer(partial, cos_tab, sin_tab, k_pos, w_query, w_key, w_value, w_out, w_gate, w_up, w_down, g1, g2, g3, g4):
+def run_layer(partial, k_pos, inv_freq, w_query, w_key, w_value, w_out, w_gate, w_up, w_down, g1, g2, g3, g4):
     seq, dim = partial.shape
     vmem = pl.BlockSpec(memory_space=pltpu.VMEM)
     hbm = pl.BlockSpec(memory_space=pl.ANY)
@@ -319,12 +424,13 @@
         layer_kernel,
         name="layer",
         out_shape=jax.ShapeDtypeStruct((seq // 4, dim), BF16),
-        in_specs=[hbm] + [vmem] * 3 + [hbm] * 7 + [vmem] * 4,
+        in_specs=[hbm] + [vmem] * 2 + [hbm] * 7 + [vmem] * 4,
         out_specs=vmem,
         scratch_shapes=[
-            pltpu.VMEM(w_query.shape, BF16), pltpu.VMEM(w_key.shape, BF16), pltpu.VMEM(w_value.shape, BF16),
+            pltpu.VMEM((dim, 512), BF16), pltpu.VMEM(w_key.shape, BF16), pltpu.VMEM(w_value.shape, BF16),
             pltpu.VMEM(w_out.shape, BF16), pltpu.VMEM(w_gate.shape, BF16), pltpu.VMEM(w_up.shape, BF16),
             pltpu.VMEM(w_down.shape, BF16),
+            pltpu.VMEM((2, WQ_ROWS, 2, 256), BF16), pltpu.VMEM((seq, 128), F32), pltpu.VMEM((seq, 128), F32),
             half_all, half_all, half_all, half_all,
             pltpu.VMEM((3, ROWS, dim), BF16),
             pltpu.VMEM((seq, 256), BF16), pltpu.VMEM((seq, 256), BF16),
@@ -332,34 +438,26 @@
             pltpu.VMEM((HALF, dim), BF16), pltpu.VMEM((HALF, dim), BF16),
             pltpu.VMEM((HALF, dim), BF16), pltpu.VMEM((2, HALF, dim), BF16),
             pltpu.VMEM((3 * HALF, dim), BF16), pltpu.VMEM((HALF, dim), BF16),
-            dma((7,)), dma((N_CHUNK,)), dma((N_CHUNK,)), dma((N_CHUNK,)), dma((N_CHUNK,)), dma((N_CHUNK,)),
+            dma((2,)), dma((6,)), dma((N_CHUNK,)), dma((N_CHUNK,)), dma((N_CHUNK,)), dma((N_CHUNK,)), dma((N_CHUNK,)),
             dma, dma, dma, dma,
             dma((N_CHUNK,)), dma((N_CHUNK,)), dma((2,)), dma((2,)), dma, dma((2,)),
             dma((3,)), dma((3,)), dma, dma,
         ],
         compiler_params=pltpu.CompilerParams(
             collective_id=0, has_side_effects=True, vmem_limit_bytes=67043328),
-    )(partial, cos_tab, sin_tab, k_pos, w_query, w_key, w_value, w_out, w_gate, w_up, w_down, g1, g2, g3, g4)
+    )(partial, k_pos, inv_freq, w_query, w_key, w_value, w_out, w_gate, w_up, w_down, g1, g2, g3, g4)
 
 
 def solution(mesh):
     in_specs = (P("dp", None), P("dp", None), P("tp", None), P(None, "tp", None), P(None, "tp", None), P(None, "tp", None), P("tp", None, None), P(None, "tp"), P(None, "tp"), P("tp", None), P(None), P(None), P(None), P(None))
 
     def device_step(tokens, positions, embed_block, w_query, w_key, w_value, w_out, w_gate, w_up, w_down, g1, g2, g3, g4):
-        dev_rank = lax.axis_index("tp")
-        vocab_local, model_dim = embed_block.shape
-        tokens, positions = tokens[0], positions[0]
-        seq = tokens.shape[0]
-        local_ids = tokens - dev_rank * vocab_local
-        in_block = (local_ids >= 0) & (local_ids < vocab_local)
-        looked = embed_block.at[lax.rem(tokens, vocab_local)].get(mode='promise_in_bounds')
-        normalizer = jnp.sqrt(jnp.float32(model_dim)).astype(BF16)
-        partial = jnp.where(in_block[:, None], looked * normalizer, jnp.zeros((), BF16))
-        inv_freq = ROPE_BASE ** (-2.0 * jnp.arange(128, dtype=F32) / 256)
-        angles = positions.astype(F32)[:, None] * inv_freq
+        model_dim = embed_block.shape[1]
+        partial = gather_rows(tokens, embed_block)
+        inv_freq = (ROPE_BASE ** (-2.0 * np.arange(128) / 256)).astype(np.float32).reshape(1, 128)
         out = run_layer(
-            partial, jnp.cos(angles), jnp.sin(angles), positions.reshape(1, seq),
-            w_query.reshape(model_dim, 512), w_key.reshape(model_dim, 256), w_value.reshape(model_dim, 256),
+            partial, positions, jnp.asarray(inv_freq),
+            w_query, w_key.reshape(model_dim, 256), w_value.reshape(model_dim, 256),
             w_out.reshape(512, model_dim), w_gate, w_up, w_down, g1, g2, g3, g4)
         return out[None]
 

time: 156 us -> 140 us (0.90)
  local copies, waits for them, and re-layouts: 16.4 us -> 2.21 us
  other arithmetic: 9.1 us -> 0 us
  Pallas kernels: 128 us -> 136 us
    pallas_call x0 -> x1, Pallas kernels: none -> 15.6 us  [gather_rows(): pl.pallas_call(functools.partial(gather_kernel, scale), name='gather', ou...]
    gather x1 -> x0, local copies, waits for them, and re-layouts: 10.5 us -> none  [device_step(): embed_block.at[lax.rem(tokens, vocab_local)].get(mode='promise_in_bounds')]
    pallas_call x1, Pallas kernels: 128 us -> 120 us  [run_layer(): pl.pallas_call(layer_kernel, name='layer', out_shape=jax.ShapeDtypeStruct...]
    select_n x2 -> x0, other arithmetic: 5.19 us -> none  [the longest x1 4.48 us: device_step(): jnp.where(in_block[:, None], looked * normalizer, jnp.zeros((), BF16))]
    unnamed x2 -> x1, local copies, waits for them, and re-layouts: 5.9 us -> 2.21 us
    sin x1 -> x0, other arithmetic: 2.49 us -> none  [device_step(): jnp.sin(angles)]
where the time goes in v3:
time: 140 us; the launch traced here: 138 us
  Pallas kernels  136 us (97%)
  local copies, waits for them, and re-layouts  2.21 us (2%)
    pallas_call x1, Pallas kernels, run_layer(): pl.pallas_call(layer_kernel, name='layer', out_shape=jax.ShapeDtypeStruct...  120 us
    pallas_call x1, Pallas kernels, gather_rows(): pl.pallas_call(functools.partial(gather_kernel, scale), name='gather', ou...  15.6 us

profile of v3, /device:TPU:0, one launch (start us, length us, event | category | flops | bytes accessed | tf_op | source)
XLA Modules:
  0.0 138.0 jit_solution(12880387741125609339)
XLA Ops:
  0.0 15.6 %gather.1.part_ref = bf16[768,2560]{1,0:T(8,128)(2,1)} custom-call(s32[1,768]{1,0:T(1,128)} %id_row_ref.1, s32[1,768]{1,0:T(1,128)} %id_row_ref.1, bf16[65552,2560]{1,0:T(8,128)(2,1)} %table_ref.1), custom_call_target="tpu_custom_call" | custom-call | tf_op jit(solution)/shard_map/gather/pallas_call | solution.py:88
  15.6 120.1 %layer.1 = bf16[192,2560]{1,0:T(8,128)(2,1)} custom-call(bf16[768,2560]{1,0:T(8,128)(2,1)} %gather.1.part_ref, s32[1,768]{1,0:T(1,128)} %kpos_ref.1, f32[1,128]{1,0:T(1,128)} %constant.2.clone.freq_ref, bf16[2560,2,256]{2,1,0:T(2,128)(2,1)} %wq_hbm.1, bf16[2560,256]{1,0:T(8,128)(2,1)} %bitcast.6, bf16[2560,256]{1,0:T(8,128)(2,1)} %bitcast.7, ...), custom_call_target="tpu_custom_call" | custom-call | tf_op jit(solution)/shard_map/layer/pallas_call | solution.py:423
  135.8 2.2 %copy.17 = bf16[1,192,2560]{2,1,0:T(8,128)(2,1)} copy(bf16[1,192,2560]{2,1,0:T(8,128)(2,1)} %bitcast.4) | data formatting | bytes 1966080

commit v4 on v2

--- a/solution.py
+++ b/solution.py
@@ -2,6 +2,7 @@
 
 import jax
 import jax.numpy as jnp
+import numpy as np
 from jax import lax
 from jax.experimental import pallas as pl
 from jax.experimental.pallas import tpu as pltpu
@@ -18,6 +19,7 @@
 HALF = 64
 SUB = 16
 N_TILE = 512
+WQ_ROWS = 256
 LEAD = 3
 LAG = 2
 LATE = 4
@@ -32,14 +34,15 @@
 
 
 def layer_kernel(
-    part_ref, cos_ref, sin_ref, kpos_ref,
+    block_rows, scale,
+    rows_ref, ids_ref, kpos_ref, freq_ref,
     wq_hbm, wk_hbm, wv_hbm, wo_hbm, wg_hbm, wu_hbm, wd_hbm,
     g1_ref, g2_ref, g3_ref, g4_ref,
     out_ref,
-    wq, wk, wv, wo, wg, wu, wd,
-    own, sib, res, y_in, norm, k_all, v_all, o_buf, h_buf, y_out, y_pair, pair_out, pair_in, z_in, stage,
-    w_sem, own_sem, sib_ss, sib_rs, ex_ss, ex_rs, a_ss, a_rs, yp_ss, yp_rs,
-    yx_ss, yx_rs, m_ss, m_rs, zp_ss, zp_rs, zx_ss, zx_rs, out_ss, out_rs,
+    wqkv, wo, wg, wu, wd,
+    wq_in, own, sib, res, y_in, norm, k_all, v_all, o_buf, h_buf, y_out, y_pair, pair_out, pair_in, z_in, stage,
+    wq_sem, w_sem, own_sem, sib_ss, sib_rs, ex_ss, ex_rs, a_ss, a_rs, yp_ss, yp_rs,
+    yx_ss, yx_rs, m_ss, m_rs, zp_ss, zp_rs, zx_ss, zx_rs, out_ss, out_rs, keep_sem,
 ):
     dp = lax.axis_index("dp")
     tp = lax.axis_index("tp")
@@ -60,11 +63,11 @@
 
     def own_copy(t):
         rows = pl.ds(pl.multiple_of(t * ROWS + core * HALF, HALF), HALF)
-        return pltpu.make_async_copy(part_ref.at[rows], own.at[half_rows(t)], own_sem.at[t])
+        return pltpu.make_async_copy(rows_ref.at[rows], own.at[half_rows(t)], own_sem.at[t])
 
     def sib_copy(t):
         rows = pl.ds(pl.multiple_of(t * ROWS + (1 - core) * HALF, HALF), HALF)
-        return remote(part_ref.at[rows], sib.at[half_rows(t)], sib_ss.at[t], sib_rs.at[t], mate)
+        return remote(rows_ref.at[rows], sib.at[half_rows(t)], sib_ss.at[t], sib_rs.at[t], mate)
 
     def ex_copy(t):
         return remote(own.at[half_rows(t)], res.at[half_rows(t)], ex_ss.at[t], ex_rs.at[t], far)
@@ -93,7 +96,7 @@
     weights = [
         pltpu.make_async_copy(src, dst, w_sem.at[i])
         for i, (src, dst) in enumerate(
-            [(wq_hbm, wq), (wk_hbm, wk), (wv_hbm, wv), (wo_hbm, wo), (wg_hbm, wg), (wu_hbm, wu), (wd_hbm, wd)])
+            [(wk_hbm, wqkv.at[:, pl.ds(512, 256)]), (wv_hbm, wqkv.at[:, pl.ds(768, 256)]), (wo_hbm, wo), (wg_hbm, wg), (wu_hbm, wu), (wd_hbm, wd)])
     ]
 
     barrier = pltpu.get_barrier_semaphore()
@@ -104,6 +107,14 @@
     for t in range(N_CHUNK):
         sib_copy(t).start()
         own_copy(t).start()
+
+    def wq_copy(i):
+        slot = lax.rem(i, 2)
+        rows = pl.ds(pl.multiple_of(i * WQ_ROWS, WQ_ROWS), WQ_ROWS)
+        return pltpu.make_async_copy(wq_hbm.at[rows], wq_in.at[slot], wq_sem.at[slot])
+
+    wq_copy(0).start()
+    wq_copy(1).start()
     for copy in weights:
         copy.start()
 
@@ -118,10 +129,23 @@
             return carry
         lax.fori_loop(0, HALF // SUB, step, 0)
 
+    def column(row_ref, t):
+        rows = pl.ds(pl.multiple_of(t * ROWS, ROWS), ROWS)
+        return jnp.broadcast_to(row_ref[:, rows], (8, ROWS)).T[:, :1]
+
     def send_embed(t, carry):
         own_copy(t).wait()
         sib_copy(t).wait_recv()
-        combine(own, sib, t * HALF, t * HALF)
+        ids = column(ids_ref, t)
+        ids = jnp.where(core == 0, ids[:HALF], ids[HALF:])
+        local, local_mate = ids - tp * block_rows, ids - mate * block_rows
+        held = (local >= 0) & (local < block_rows)
+        held_mate = (local_mate >= 0) & (local_mate < block_rows)
+        for r in range(0, HALF, SUB):
+            part = slice(r, r + SUB)
+            rows = pl.ds(pl.multiple_of(t * HALF + r, SUB), SUB)
+            looked = jnp.where(held[part], own[rows, :].astype(F32), jnp.where(held_mate[part], sib[rows, :].astype(F32), 0.0))
+            own[rows, :] = (looked * scale).astype(BF16)
 
         @pl.when(t < LEAD)
         def _():
@@ -132,9 +156,29 @@
     k_all[...] = jnp.zeros_like(k_all)
     v_all[...] = jnp.zeros_like(v_all)
     gain1, gain2, gain3, gain4 = [(1.0 + g[...]).reshape(1, -1) for g in (g1_ref, g2_ref, g3_ref, g4_ref)]
+
+    out_row = lax.broadcasted_iota(jnp.int32, (256, 256), 0)
+    in_row = lax.broadcasted_iota(jnp.int32, (256, 256), 1)
+    split_heads = jnp.where(in_row == jnp.where(out_row < 128, 2 * out_row, 2 * out_row - 255), 1.0, 0.0).astype(BF16)
+
+    def spread_wq(i, carry):
+        slot = lax.rem(i, 2)
+        wq_copy(i).wait()
+        for r in range(0, WQ_ROWS, 128):
+            rows = pl.ds(pl.multiple_of(i * WQ_ROWS + r, 128), 128)
+            both = wq_in[slot, r:r + 128].reshape(256, 256)
+            both = jnp.dot(split_heads, both, preferred_element_type=F32).astype(BF16)
+            wqkv[rows, :256] = both[:128]
+            wqkv[rows, 256:512] = both[128:]
+
+        @pl.when(i + 2 < 2560 // WQ_ROWS)
+        def _():
+            wq_copy(i + 2).start()
+        return carry
+    lax.fori_loop(0, 2560 // WQ_ROWS, spread_wq, 0)
     for t in range(N_CHUNK):
         sib_copy(t).wait_send()
-    for copy in weights[:4]:
+    for copy in weights[:3]:
         copy.wait()
 
     def rope(states, cos_tab, sin_tab):
@@ -145,34 +189,45 @@
         top, bottom = both[:HALF], both[HALF:]
         return jnp.where(core == 0, top, bottom), jnp.where(core == 0, bottom, top)
 
-    def attention_chunk(t):
+    def a_copy(t):
+        slot = lax.rem(t, 2)
+        return norm_copy(2 + slot, a_ss.at[slot], a_rs.at[slot])
+
+    def embed_in(t):
         base = t * HALF
+        slot = 2 + lax.rem(t, 2)
         ex_copy(t).wait_recv()
 
         def embed_step(i, c):
             rows = sub_rows(base, i)
             embed = own[rows, :].astype(F32) + res[rows, :].astype(F32)
             res[rows, :] = embed.astype(BF16)
-            norm[2, sub_rows(core * HALF, i), :] = rms(embed, gain1).astype(BF16)
+            norm[slot, sub_rows(core * HALF, i), :] = rms(embed, gain1).astype(BF16)
             return c
         lax.fori_loop(0, HALF // SUB, embed_step, 0)
-
-        copy = norm_copy(2, a_ss, a_rs)
-        copy.start()
-        copy.wait()
-        act = norm[2]
+        a_copy(t).start()
+
+    def attention_chunk(t):
+        slot = 2 + lax.rem(t, 2)
         rows = pl.ds(pl.multiple_of(t * ROWS, ROWS), ROWS)
-        cos_tab, sin_tab = cos_ref[rows, :], sin_ref[rows, :]
-        lower, upper = rope(jnp.dot(act, wk[...], preferred_element_type=F32), cos_tab, sin_tab)
+
+        @pl.when(t <= LAG)
+        def _():
+            embed_in(t)
+        q_pos = column(kpos_ref, t)
+        angles = q_pos.astype(F32) * freq_ref[...]
+        cos_tab, sin_tab = jnp.cos(angles), jnp.sin(angles)
+        offset = q_pos - kpos_ref[...]
+        keep = (offset >= 0) & (offset < WINDOW)
+        a_copy(t).wait()
+        proj = jnp.dot(norm[slot], wqkv[:, 512:], preferred_element_type=F32)
+        lower, upper = rope(proj[:, :256], cos_tab, sin_tab)
         k_all[rows, :128] = lower.astype(BF16)
         k_all[rows, 128:] = upper.astype(BF16)
-        v_all[rows, :] = jnp.dot(act, wv[...], preferred_element_type=F32).astype(BF16)
-        q_pos = jnp.broadcast_to(kpos_ref[:, rows], (8, ROWS)).T[:, :1]
-        offset = q_pos - kpos_ref[...]
-        keep = (offset >= 0) & (offset < WINDOW)
+        v_all[rows, :] = proj[:, 256:].astype(BF16)
+        proj = jnp.dot(norm[slot], wqkv[:, :512], preferred_element_type=F32)
         for head in range(2):
-            proj = jnp.dot(act, wq[:, head * 256:(head + 1) * 256], preferred_element_type=F32)
-            lower, upper = rope(proj, cos_tab, sin_tab)
+            lower, upper = rope(proj[:, head * 256:(head + 1) * 256], cos_tab, sin_tab)
             query = jnp.concatenate([(lower * QUERY_SCALE).astype(BF16), (upper * QUERY_SCALE).astype(BF16)], axis=-1)
             scores = lax.dot_general(query, k_all[...], (((1,), (1,)), ((), ())), preferred_element_type=F32)
             weight = jnp.where(keep, jnp.exp(SOFT_CAP * jnp.tanh(scores * (1.0 / SOFT_CAP))), 0.0)
@@ -186,10 +241,11 @@
             sib[half_rows(t), cols], y_out[:, cols] = split_halves(both)
             return c
         lax.fori_loop(0, 2560 // N_TILE, out_tile, 0, unroll=True)
-        copy = yp_copy()
-        copy.start()
-        copy.wait()
-        combine(sib, y_pair, base, 0)
+        yp_copy().start()
+
+    def send_proj(t):
+        yp_copy().wait()
+        combine(sib, y_pair, t * HALF, 0)
         yx_copy(t).start()
 
         @pl.when(t + LEAD < N_CHUNK)
@@ -215,20 +271,16 @@
         zp_copy(t).wait_recv()
         combine(own, pair_in.at[lax.rem(t, 2)], t * HALF, 0)
 
-        @pl.when(lax.div(t, 3) != chip)
+        @pl.when((lax.div(t, 3) != chip) & (t >= LAG))
         def _():
             zx_copy(t).start()
 
     def mlp_chunk(t):
         slot = lax.rem(t, 2)
 
-        @pl.when(t < LATE)
-        def _():
-            mlp_in(t)
-
         @pl.when(t == 0)
         def _():
-            for copy in weights[4:]:
+            for copy in weights[3:]:
                 copy.wait()
         ex_copy(t).wait_send()
         m_copy(t).wait()
@@ -245,6 +297,10 @@
         def _():
             finish_pair(t - 1)
 
+        @pl.when(t + LAG + 1 < N_CHUNK)
+        def _():
+            embed_in(t + LAG + 1)
+
         @pl.when((t + 1 >= LATE) & (t < N_CHUNK - 1))
         def _():
             mlp_in(t + 1)
@@ -266,6 +322,19 @@
         def _():
             attention_chunk(s)
 
+        @pl.when((s >= LAG) & (s < LATE + LAG))
+        def _():
+            mlp_in(s - LAG)
+
+        @pl.when(s < N_CHUNK)
+        def _():
+            send_proj(s)
+
+        @pl.when((s == N_CHUNK - 1) & (chip != 0))
+        def _():
+            for t in range(LAG):
+                zx_copy(t).start()
+
         @pl.when(s >= LAG)
         def _():
             mlp_chunk(s - LAG)
@@ -273,7 +342,7 @@
     lax.fori_loop(0, N_CHUNK + LAG, step, 0)
     finish_pair(N_CHUNK - 1)
 
-    def result(j, dst, dst_base):
+    def result(j):
         t = 3 * chip + j
         zx_copy(j).wait_recv()
 
@@ -281,27 +350,30 @@
             rows = sub_rows(t * HALF, i)
             proj = (own[rows, :].astype(F32) + z_in[sub_rows(j * HALF, i), :].astype(F32)).astype(BF16).astype(F32)
             final = res[rows, :].astype(F32) + rms(proj, gain4).astype(BF16).astype(F32)
-            dst[sub_rows(dst_base, i), :] = final.astype(BF16)
+            stage[sub_rows(j * HALF, i), :] = final.astype(BF16)
             return c
         lax.fori_loop(0, HALF // SUB, step, 0)
 
-    handover = remote(stage, out_ref.at[pl.ds(HALF, HALF)], out_ss, out_rs, mate)
-
-    @pl.when(core == 0)
-    def _():
-        result(0, out_ref, 0)
-        result(1, out_ref, 2 * HALF)
-        result(2, stage, 0)
-        handover.start()
-
-    @pl.when(core == 1)
-    def _():
-        result(0, stage, 0)
-        handover.start()
-        result(1, out_ref, 0)
-        result(2, out_ref, 2 * HALF)
-
-    handover.wait()
+    def keep_copy(j, place):
+        return pltpu.make_async_copy(stage.at[pl.ds(j * HALF, HALF)], out_ref.at[pl.ds(place * HALF, HALF)], keep_sem.at[place // 2])
+
+    def give_copy(j):
+        return remote(stage.at[pl.ds(j * HALF, HALF)], out_ref.at[pl.ds(HALF, HALF)], out_ss, out_rs, mate)
+
+    for j in range(3):
+        result(j)
+
+        @pl.when(core == 0)
+        def _():
+            (give_copy(j) if j == 2 else keep_copy(j, 2 * j)).start()
+
+        @pl.when(core == 1)
+        def _():
+            (give_copy(j) if j == 0 else keep_copy(j, 2 * j - 2)).start()
+
+    give_copy(0).wait()
+    keep_copy(0, 0).wait()
+    keep_copy(0, 2).wait()
     zp_copy(N_CHUNK - 1).wait_send()
     for t in range(N_CHUNK):
         yx_copy(t).wait_send()
@@ -309,57 +381,52 @@
         zx_copy(3 * (1 - chip) + j).wait_send()
 
 
-def run_layer(partial, cos_tab, sin_tab, k_pos, w_query, w_key, w_value, w_out, w_gate, w_up, w_down, g1, g2, g3, g4):
-    seq, dim = partial.shape
+def run_layer(block_rows, looked, tokens, k_pos, inv_freq, w_query, w_key, w_value, w_out, w_gate, w_up, w_down, g1, g2, g3, g4):
+    seq, dim = looked.shape
+    scale = float(np.sqrt(np.float32(dim)).astype(jnp.bfloat16))
     vmem = pl.BlockSpec(memory_space=pltpu.VMEM)
     hbm = pl.BlockSpec(memory_space=pl.ANY)
     half_all = pltpu.VMEM((seq // 2, dim), BF16)
     dma = pltpu.SemaphoreType.DMA
     return pl.pallas_call(
-        layer_kernel,
+        functools.partial(layer_kernel, block_rows, scale),
         name="layer",
         out_shape=jax.ShapeDtypeStruct((seq // 4, dim), BF16),
         in_specs=[hbm] + [vmem] * 3 + [hbm] * 7 + [vmem] * 4,
-        out_specs=vmem,
+        out_specs=hbm,
         scratch_shapes=[
-            pltpu.VMEM(w_query.shape, BF16), pltpu.VMEM(w_key.shape, BF16), pltpu.VMEM(w_value.shape, BF16),
+            pltpu.VMEM((dim, 1024), BF16),
             pltpu.VMEM(w_out.shape, BF16), pltpu.VMEM(w_gate.shape, BF16), pltpu.VMEM(w_up.shape, BF16),
             pltpu.VMEM(w_down.shape, BF16),
+            pltpu.VMEM((2, WQ_ROWS, 2, 256), BF16),
             half_all, half_all, half_all, half_all,
-            pltpu.VMEM((3, ROWS, dim), BF16),
+            pltpu.VMEM((4, ROWS, dim), BF16),
             pltpu.VMEM((seq, 256), BF16), pltpu.VMEM((seq, 256), BF16),
             pltpu.VMEM((ROWS, 512), BF16), pltpu.VMEM((ROWS, dim), BF16),
             pltpu.VMEM((HALF, dim), BF16), pltpu.VMEM((HALF, dim), BF16),
             pltpu.VMEM((HALF, dim), BF16), pltpu.VMEM((2, HALF, dim), BF16),
-            pltpu.VMEM((3 * HALF, dim), BF16), pltpu.VMEM((HALF, dim), BF16),
-            dma((7,)), dma((N_CHUNK,)), dma((N_CHUNK,)), dma((N_CHUNK,)), dma((N_CHUNK,)), dma((N_CHUNK,)),
-            dma, dma, dma, dma,
+            pltpu.VMEM((3 * HALF, dim), BF16), pltpu.VMEM((3 * HALF, dim), BF16),
+            dma((2,)), dma((6,)), dma((N_CHUNK,)), dma((N_CHUNK,)), dma((N_CHUNK,)), dma((N_CHUNK,)), dma((N_CHUNK,)),
+            dma((2,)), dma((2,)), dma, dma,
             dma((N_CHUNK,)), dma((N_CHUNK,)), dma((2,)), dma((2,)), dma, dma((2,)),
-            dma((3,)), dma((3,)), dma, dma,
+            dma((3,)), dma((3,)), dma, dma, dma((2,)),
         ],
         compiler_params=pltpu.CompilerParams(
             collective_id=0, has_side_effects=True, vmem_limit_bytes=67043328),
-    )(partial, cos_tab, sin_tab, k_pos, w_query, w_key, w_value, w_out, w_gate, w_up, w_down, g1, g2, g3, g4)
+    )(looked, tokens, k_pos, inv_freq, w_query, w_key, w_value, w_out, w_gate, w_up, w_down, g1, g2, g3, g4)
 
 
 def solution(mesh):
     in_specs = (P("dp", None), P("dp", None), P("tp", None), P(None, "tp", None), P(None, "tp", None), P(None, "tp", None), P("tp", None, None), P(None, "tp"), P(None, "tp"), P("tp", None), P(None), P(None), P(None), P(None))
 
     def device_step(tokens, positions, embed_block, w_query, w_key, w_value, w_out, w_gate, w_up, w_down, g1, g2, g3, g4):
-        dev_rank = lax.axis_index("tp")
-        vocab_local, model_dim = embed_block.shape
-        tokens, positions = tokens[0], positions[0]
-        seq = tokens.shape[0]
-        local_ids = tokens - dev_rank * vocab_local
-        in_block = (local_ids >= 0) & (local_ids < vocab_local)
-        looked = embed_block.at[lax.rem(tokens, vocab_local)].get(mode='promise_in_bounds')
-        normalizer = jnp.sqrt(jnp.float32(model_dim)).astype(BF16)
-        partial = jnp.where(in_block[:, None], looked * normalizer, jnp.zeros((), BF16))
-        inv_freq = ROPE_BASE ** (-2.0 * jnp.arange(128, dtype=F32) / 256)
-        angles = positions.astype(F32)[:, None] * inv_freq
+        model_dim = embed_block.shape[1]
+        block_rows = embed_block.shape[0]
+        looked = embed_block.at[lax.rem(tokens[0], block_rows)].get(mode='promise_in_bounds')
+        inv_freq = (ROPE_BASE ** (-2.0 * np.arange(128) / 256)).astype(np.float32).reshape(1, 128)
         out = run_layer(
-            partial, jnp.cos(angles), jnp.sin(angles), positions.reshape(1, seq),
-            w_query.reshape(model_dim, 512), w_key.reshape(model_dim, 256), w_value.reshape(model_dim, 256),
+            block_rows, looked, tokens, positions, jnp.asarray(inv_freq),
+            w_query, w_key.reshape(model_dim, 256), w_value.reshape(model_dim, 256),
             w_out.reshape(512, model_dim), w_gate, w_up, w_down, g1, g2, g3, g4)
         return out[None]
 

time: 156 us -> 130 us (0.83); the launches traced: 154 us -> 130 us
  Pallas kernels: 128 us -> 116 us
  other arithmetic: 9.1 us -> 0.71 us
  local copies, waits for them, and re-layouts: 16.4 us -> 12.7 us
    pallas_call x1, Pallas kernels: 128 us -> 116 us  [run_layer(): pl.pallas_call(functools.partial(layer_kernel, block_rows, scale), name='...]
    select_n x2 -> x1, other arithmetic: 5.19 us -> 0.71 us  [device_step(): embed_block.at[lax.rem(tokens[0], block_rows)].get(mode='promise_in_bounds')]
    unnamed x2 -> x1, local copies, waits for them, and re-layouts: 5.9 us -> 2.21 us
    sin x1 -> x0, other arithmetic: 2.49 us -> none  [device_step(): jnp.sin(angles)]
where the time goes in v4:
time: 130 us
  Pallas kernels  116 us (89%)
  local copies, waits for them, and re-layouts  12.7 us (10%)
    pallas_call x1, Pallas kernels, run_layer(): pl.pallas_call(functools.partial(layer_kernel, block_rows, scale), name='...  116 us
    gather x1, local copies, waits for them, and re-layouts, device_step(): embed_block.at[lax.rem(tokens[0], block_rows)].get(mode='promise_in_bounds')  10.5 us

profile of v4, /device:TPU:0, one launch (start us, length us, event | category | flops | bytes accessed | tf_op | source)
XLA Modules:
  0.0 129.6 jit_solution(10812370462711132593)
XLA Ops:
  0.0 0.7 fusion
  0.7 10.5 %gather_fusion = bf16[768,2560]{1,0:T(8,128)(2,1)} fusion(bf16[65552,2560]{1,0:T(8,128)(2,1)} %param.17, s32[1024]{0:T(1024)S(1)} %pad_clamp_fusion), kind=kCustom, calls=%fused_computation | custom fusion | bytes 7867392 | tf_op jit(solution)/shard_map/gather | solution.py:425
  11.2 116.2 %layer.1 = bf16[192,2560]{1,0:T(8,128)(2,1)} custom-call(bf16[768,2560]{1,0:T(8,128)(2,1)} %gather_fusion, s32[1,768]{1,0:T(1,128)} %ids_ref.1, s32[1,768]{1,0:T(1,128)} %kpos_ref.1, f32[1,128]{1,0:T(1,128)} %constant.6.clone.freq_ref, bf16[2560,2,256]{2,1,0:T(2,128)(2,1)} %wq_hbm.1, bf16[2560,256]{1,0:T(8,128)(2,1)} %bitcast.8, bf16[2560,256]{1,0:T(8,128)(2,1)} %bitcast.9, ...), custom_call_target="tpu_custom_call" | custom-call | tf_op jit(solution)/shard_map/layer/pallas_call | solution.py:391
  127.4 2.2 %copy.17 = bf16[1,192,2560]{2,1,0:T(8,128)(2,1)} copy(bf16[1,192,2560]{2,1,0:T(8,128)(2,1)} %bitcast.6) | data formatting | bytes 1966080
  (1 shorter events, 0.0 us)

commit v5 on v4

--- a/solution.py
+++ b/solution.py
@@ -18,8 +18,10 @@
 ROWS = 128
 HALF = 64
 SUB = 16
+PIECES = 4
 N_TILE = 512
 WQ_ROWS = 256
+EARLY = 2
 LEAD = 3
 LAG = 2
 LATE = 4
@@ -43,6 +45,7 @@
     wq_in, own, sib, res, y_in, norm, k_all, v_all, o_buf, h_buf, y_out, y_pair, pair_out, pair_in, z_in, stage,
     wq_sem, w_sem, own_sem, sib_ss, sib_rs, ex_ss, ex_rs, a_ss, a_rs, yp_ss, yp_rs,
     yx_ss, yx_rs, m_ss, m_rs, zp_ss, zp_rs, zx_ss, zx_rs, out_ss, out_rs, keep_sem,
+    stage_sem, first_ss, first_rs, ex0_ss, ex0_rs,
 ):
     dp = lax.axis_index("dp")
     tp = lax.axis_index("tp")
@@ -69,6 +72,19 @@
         rows = pl.ds(pl.multiple_of(t * ROWS + (1 - core) * HALF, HALF), HALF)
         return remote(rows_ref.at[rows], sib.at[half_rows(t)], sib_ss.at[t], sib_rs.at[t], mate)
 
+    def piece_rows(i, base=0):
+        return pl.ds(pl.multiple_of(base + i * SUB, SUB), SUB)
+
+    def stage_copy(i):
+        rows = pl.ds(pl.multiple_of((1 - core) * HALF + i * SUB, SUB), SUB)
+        return pltpu.make_async_copy(rows_ref.at[rows], y_out.at[piece_rows(i)], stage_sem.at[i])
+
+    def sib_first(i):
+        return remote(y_out.at[piece_rows(i)], sib.at[piece_rows(i)], first_ss.at[i], first_rs.at[i], mate)
+
+    def ex_first(i):
+        return remote(own.at[piece_rows(i)], res.at[piece_rows(i)], ex0_ss.at[i], ex0_rs.at[i], far)
+
     def ex_copy(t):
         return remote(own.at[half_rows(t)], res.at[half_rows(t)], ex_ss.at[t], ex_rs.at[t], far)
 
@@ -89,9 +105,9 @@
         slot = lax.rem(t, 2)
         return remote(pair_out, pair_in.at[slot], zp_ss, zp_rs.at[slot], mate)
 
-    def zx_copy(t):
+    def zx_copy(t, i):
         j = lax.rem(t, 3)
-        return remote(own.at[half_rows(t)], z_in.at[half_rows(j)], zx_ss.at[j], zx_rs.at[j], far)
+        return remote(own.at[piece_rows(i, t * HALF)], z_in.at[piece_rows(i, j * HALF)], zx_ss.at[j, i], zx_rs.at[j, i], far)
 
     weights = [
         pltpu.make_async_copy(src, dst, w_sem.at[i])
@@ -99,12 +115,18 @@
             [(wk_hbm, wqkv.at[:, pl.ds(512, 256)]), (wv_hbm, wqkv.at[:, pl.ds(768, 256)]), (wo_hbm, wo), (wg_hbm, wg), (wu_hbm, wu), (wd_hbm, wd)])
     ]
 
+    for i in range(PIECES):
+        stage_copy(i).start()
+    own_copy(0).start()
     barrier = pltpu.get_barrier_semaphore()
     for peer in (mate, far):
         pl.semaphore_signal(barrier, inc=1, device_id=(dp, peer), device_id_type=MESH)
     pl.semaphore_wait(barrier, 2)
 
-    for t in range(N_CHUNK):
+    for i in range(PIECES):
+        stage_copy(i).wait()
+        sib_first(i).start()
+    for t in range(1, N_CHUNK):
         sib_copy(t).start()
         own_copy(t).start()
 
@@ -115,7 +137,7 @@
 
     wq_copy(0).start()
     wq_copy(1).start()
-    for copy in weights:
+    for copy in weights[:3]:
         copy.start()
 
     def sub_rows(base, i):
@@ -133,25 +155,39 @@
         rows = pl.ds(pl.multiple_of(t * ROWS, ROWS), ROWS)
         return jnp.broadcast_to(row_ref[:, rows], (8, ROWS)).T[:, :1]
 
-    def send_embed(t, carry):
-        own_copy(t).wait()
-        sib_copy(t).wait_recv()
+    def owners(t):
         ids = column(ids_ref, t)
         ids = jnp.where(core == 0, ids[:HALF], ids[HALF:])
         local, local_mate = ids - tp * block_rows, ids - mate * block_rows
         held = (local >= 0) & (local < block_rows)
         held_mate = (local_mate >= 0) & (local_mate < block_rows)
+        return held, held_mate
+
+    def pick_rows(rows, held, held_mate):
+        looked = jnp.where(held, own[rows, :].astype(F32), jnp.where(held_mate, sib[rows, :].astype(F32), 0.0))
+        own[rows, :] = (looked * scale).astype(BF16)
+
+    held, held_mate = owners(0)
+    own_copy(0).wait()
+    for i in range(PIECES):
+        part = slice(i * SUB, (i + 1) * SUB)
+        sib_first(i).wait_recv()
+        pick_rows(pl.ds(i * SUB, SUB), held[part], held_mate[part])
+        ex_first(i).start()
+
+    def send_embed(t, carry):
+        held, held_mate = owners(t)
+        own_copy(t).wait()
+        sib_copy(t).wait_recv()
         for r in range(0, HALF, SUB):
             part = slice(r, r + SUB)
-            rows = pl.ds(pl.multiple_of(t * HALF + r, SUB), SUB)
-            looked = jnp.where(held[part], own[rows, :].astype(F32), jnp.where(held_mate[part], sib[rows, :].astype(F32), 0.0))
-            own[rows, :] = (looked * scale).astype(BF16)
+            pick_rows(pl.ds(pl.multiple_of(t * HALF + r, SUB), SUB), held[part], held_mate[part])
 
         @pl.when(t < LEAD)
         def _():
             ex_copy(t).start()
         return carry
-    lax.fori_loop(0, N_CHUNK, send_embed, 0)
+    lax.fori_loop(1, N_CHUNK, send_embed, 0)
 
     k_all[...] = jnp.zeros_like(k_all)
     v_all[...] = jnp.zeros_like(v_all)
@@ -176,7 +212,11 @@
             wq_copy(i + 2).start()
         return carry
     lax.fori_loop(0, 2560 // WQ_ROWS, spread_wq, 0)
-    for t in range(N_CHUNK):
+    for copy in weights[3:]:
+        copy.start()
+    for i in range(PIECES):
+        sib_first(i).wait_send()
+    for t in range(1, N_CHUNK):
         sib_copy(t).wait_send()
     for copy in weights[:3]:
         copy.wait()
@@ -196,7 +236,15 @@
     def embed_in(t):
         base = t * HALF
         slot = 2 + lax.rem(t, 2)
-        ex_copy(t).wait_recv()
+
+        @pl.when(t == 0)
+        def _():
+            for i in range(PIECES):
+                ex_first(i).wait_recv()
+
+        @pl.when(t > 0)
+        def _():
+            ex_copy(t).wait_recv()
 
         def embed_step(i, c):
             rows = sub_rows(base, i)
@@ -273,7 +321,8 @@
 
         @pl.when((lax.div(t, 3) != chip) & (t >= LAG))
         def _():
-            zx_copy(t).start()
+            for i in range(PIECES):
+                zx_copy(t, i).start()
 
     def mlp_chunk(t):
         slot = lax.rem(t, 2)
@@ -282,7 +331,12 @@
         def _():
             for copy in weights[3:]:
                 copy.wait()
-        ex_copy(t).wait_send()
+            for i in range(PIECES):
+                ex_first(i).wait_send()
+
+        @pl.when(t > 0)
+        def _():
+            ex_copy(t).wait_send()
         m_copy(t).wait()
 
         def gate_tile(n, c):
@@ -291,11 +345,12 @@
             up = jnp.dot(norm[slot], wu[:, cols], preferred_element_type=F32)
             h_buf[:, cols] = (jax.nn.gelu(gate, approximate=True) * up).astype(BF16)
             return c
-        lax.fori_loop(0, 2560 // N_TILE, gate_tile, 0, unroll=True)
+        lax.fori_loop(0, EARLY, gate_tile, 0, unroll=True)
 
         @pl.when(t > 0)
         def _():
             finish_pair(t - 1)
+        lax.fori_loop(EARLY, 2560 // N_TILE, gate_tile, 0, unroll=True)
 
         @pl.when(t + LAG + 1 < N_CHUNK)
         def _():
@@ -333,7 +388,8 @@
         @pl.when((s == N_CHUNK - 1) & (chip != 0))
         def _():
             for t in range(LAG):
-                zx_copy(t).start()
+                for i in range(PIECES):
+                    zx_copy(t, i).start()
 
         @pl.when(s >= LAG)
         def _():
@@ -342,43 +398,41 @@
     lax.fori_loop(0, N_CHUNK + LAG, step, 0)
     finish_pair(N_CHUNK - 1)
 
-    def result(j):
-        t = 3 * chip + j
-        zx_copy(j).wait_recv()
-
+    def keep_copy(j, place, i):
+        rows = piece_rows(i, j * HALF)
+        return pltpu.make_async_copy(stage.at[rows], out_ref.at[piece_rows(i, place * HALF)], keep_sem.at[place // 2, i])
+
+    def give_copy(j, i):
+        return remote(stage.at[piece_rows(i, j * HALF)], out_ref.at[piece_rows(i, HALF)], out_ss.at[i], out_rs.at[i], mate)
+
+    for j in range(3):
         def step(i, c):
-            rows = sub_rows(t * HALF, i)
+            zx_copy(j, i).wait_recv()
+            rows = sub_rows((3 * chip + j) * HALF, i)
             proj = (own[rows, :].astype(F32) + z_in[sub_rows(j * HALF, i), :].astype(F32)).astype(BF16).astype(F32)
             final = res[rows, :].astype(F32) + rms(proj, gain4).astype(BF16).astype(F32)
             stage[sub_rows(j * HALF, i), :] = final.astype(BF16)
-            return c
-        lax.fori_loop(0, HALF // SUB, step, 0)
-
-    def keep_copy(j, place):
-        return pltpu.make_async_copy(stage.at[pl.ds(j * HALF, HALF)], out_ref.at[pl.ds(place * HALF, HALF)], keep_sem.at[place // 2])
-
-    def give_copy(j):
-        return remote(stage.at[pl.ds(j * HALF, HALF)], out_ref.at[pl.ds(HALF, HALF)], out_ss, out_rs, mate)
-
-    for j in range(3):
-        result(j)
-
-        @pl.when(core == 0)
-        def _():
-            (give_copy(j) if j == 2 else keep_copy(j, 2 * j)).start()
-
-        @pl.when(core == 1)
-        def _():
-            (give_copy(j) if j == 0 else keep_copy(j, 2 * j - 2)).start()
-
-    give_copy(0).wait()
-    keep_copy(0, 0).wait()
-    keep_copy(0, 2).wait()
+
+            @pl.when(core == 0)
+            def _():
+                (give_copy(j, i) if j == 2 else keep_copy(j, 2 * j, i)).start()
+
+            @pl.when(core == 1)
+            def _():
+                (give_copy(j, i) if j == 0 else keep_copy(j, 2 * j - 2, i)).start()
+            return c
+        lax.fori_loop(0, PIECES, step, 0)
+
+    for i in range(PIECES):
+        give_copy(0, i).wait()
+        keep_copy(0, 0, i).wait()
+        keep_copy(0, 2, i).wait()
     zp_copy(N_CHUNK - 1).wait_send()
     for t in range(N_CHUNK):
         yx_copy(t).wait_send()
     for j in range(3):
-        zx_copy(3 * (1 - chip) + j).wait_send()
+        for i in range(PIECES):
+            zx_copy(3 * (1 - chip) + j, i).wait_send()
 
 
 def run_layer(block_rows, looked, tokens, k_pos, inv_freq, w_query, w_key, w_value, w_out, w_gate, w_up, w_down, g1, g2, g3, g4):
@@ -409,7 +463,8 @@
             dma((2,)), dma((6,)), dma((N_CHUNK,)), dma((N_CHUNK,)), dma((N_CHUNK,)), dma((N_CHUNK,)), dma((N_CHUNK,)),
             dma((2,)), dma((2,)), dma, dma,
             dma((N_CHUNK,)), dma((N_CHUNK,)), dma((2,)), dma((2,)), dma, dma((2,)),
-            dma((3,)), dma((3,)), dma, dma, dma((2,)),
+            dma((3, PIECES)), dma((3, PIECES)), dma((PIECES,)), dma((PIECES,)), dma((2, PIECES)),
+            dma((PIECES,)), dma((PIECES,)), dma((PIECES,)), dma((PIECES,)), dma((PIECES,)),
         ],
         compiler_params=pltpu.CompilerParams(
             collective_id=0, has_side_effects=True, vmem_limit_bytes=67043328),

time: 130 us -> 129 us (level)
    pallas_call x1, Pallas kernels: 116 us -> 115 us  [run_layer(): pl.pallas_call(functools.partial(layer_kernel, block_rows, scale), name='...]
where the time goes in v5:
time: 129 us; the launch traced here: 128 us
  Pallas kernels  115 us (89%)
  local copies, waits for them, and re-layouts  12.7 us (10%)
    pallas_call x1, Pallas kernels, run_layer(): pl.pallas_call(functools.partial(layer_kernel, block_rows, scale), name='...  115 us
    gather x1, local copies, waits for them, and re-layouts, device_step(): embed_block.at[lax.rem(tokens[0], block_rows)].get(mode='promise_in_bounds')  10.5 us

profile of v5, /device:TPU:0, one launch (start us, length us, event | category | flops | bytes accessed | tf_op | source)
XLA Modules:
  0.0 128.2 jit_solution(1569324661127749328)
XLA Ops:
  0.0 0.7 fusion
  0.7 10.5 %gather_fusion = bf16[768,2560]{1,0:T(8,128)(2,1)} fusion(bf16[65552,2560]{1,0:T(8,128)(2,1)} %param.17, s32[1024]{0:T(1024)S(1)} %pad_clamp_fusion), kind=kCustom, calls=%fused_computation | custom fusion | bytes 7867392 | tf_op jit(solution)/shard_map/gather | solution.py:480
  11.2 114.8 %layer.1 = bf16[192,2560]{1,0:T(8,128)(2,1)} custom-call(bf16[768,2560]{1,0:T(8,128)(2,1)} %gather_fusion, s32[1,768]{1,0:T(1,128)} %ids_ref.1, s32[1,768]{1,0:T(1,128)} %kpos_ref.1, f32[1,128]{1,0:T(1,128)} %constant.6.clone.freq_ref, bf16[2560,2,256]{2,1,0:T(2,128)(2,1)} %wq_hbm.1, bf16[2560,256]{1,0:T(8,128)(2,1)} %bitcast.8, bf16[2560,256]{1,0:T(8,128)(2,1)} %bitcast.9, ...), custom_call_target="tpu_custom_call" | custom-call | tf_op jit(solution)/shard_map/layer/pallas_call | solution.py:445
  126.0 2.2 %copy.17 = bf16[1,192,2560]{2,1,0:T(8,128)(2,1)} copy(bf16[1,192,2560]{2,1,0:T(8,128)(2,1)} %bitcast.6) | data formatting | bytes 1966080
  (1 shorter events, 0.0 us)

commit v6 on v5

--- a/solution.py
+++ b/solution.py
@@ -37,15 +37,16 @@
 
 def layer_kernel(
     block_rows, scale,
-    rows_ref, ids_ref, kpos_ref, freq_ref,
+    rows_ref, ids_hbm, kpos_hbm, freq_hbm,
     wq_hbm, wk_hbm, wv_hbm, wo_hbm, wg_hbm, wu_hbm, wd_hbm,
-    g1_ref, g2_ref, g3_ref, g4_ref,
+    g1_hbm, g2_hbm, g3_hbm, g4_hbm,
     out_ref,
+    ids_ref, kpos_ref, freq_ref, g1_ref, g2_ref, g3_ref, g4_ref,
     wqkv, wo, wg, wu, wd,
     wq_in, own, sib, res, y_in, norm, k_all, v_all, o_buf, h_buf, y_out, y_pair, pair_out, pair_in, z_in, stage,
     wq_sem, w_sem, own_sem, sib_ss, sib_rs, ex_ss, ex_rs, a_ss, a_rs, yp_ss, yp_rs,
     yx_ss, yx_rs, m_ss, m_rs, zp_ss, zp_rs, zx_ss, zx_rs, out_ss, out_rs, keep_sem,
-    stage_sem, first_ss, first_rs, ex0_ss, ex0_rs,
+    small_sem, stage_sem, first_ss, first_rs, ex0_ss, ex0_rs,
 ):
     dp = lax.axis_index("dp")
     tp = lax.axis_index("tp")
@@ -118,6 +119,14 @@
     for i in range(PIECES):
         stage_copy(i).start()
     own_copy(0).start()
+    small = [
+        pltpu.make_async_copy(src, dst, small_sem.at[i])
+        for i, (src, dst) in enumerate([
+            (ids_hbm, ids_ref), (kpos_hbm, kpos_ref), (freq_hbm, freq_ref),
+            (g1_hbm, g1_ref), (g2_hbm, g2_ref), (g3_hbm, g3_ref), (g4_hbm, g4_ref)])
+    ]
+    for copy in small:
+        copy.start()
     barrier = pltpu.get_barrier_semaphore()
     for peer in (mate, far):
         pl.semaphore_signal(barrier, inc=1, device_id=(dp, peer), device_id_type=MESH)
@@ -167,6 +176,7 @@
         looked = jnp.where(held, own[rows, :].astype(F32), jnp.where(held_mate, sib[rows, :].astype(F32), 0.0))
         own[rows, :] = (looked * scale).astype(BF16)
 
+    small[0].wait()
     held, held_mate = owners(0)
     own_copy(0).wait()
     for i in range(PIECES):
@@ -189,6 +199,8 @@
         return carry
     lax.fori_loop(1, N_CHUNK, send_embed, 0)
 
+    for copy in small[1:]:
+        copy.wait()
     k_all[...] = jnp.zeros_like(k_all)
     v_all[...] = jnp.zeros_like(v_all)
     gain1, gain2, gain3, gain4 = [(1.0 + g[...]).reshape(1, -1) for g in (g1_ref, g2_ref, g3_ref, g4_ref)]
@@ -324,6 +336,12 @@
             for i in range(PIECES):
                 zx_copy(t, i).start()
 
+        @pl.when((t == LAG) & (chip != 0))
+        def _():
+            for early in range(LAG):
+                for i in range(PIECES):
+                    zx_copy(early, i).start()
+
     def mlp_chunk(t):
         slot = lax.rem(t, 2)
 
@@ -385,12 +403,6 @@
         def _():
             send_proj(s)
 
-        @pl.when((s == N_CHUNK - 1) & (chip != 0))
-        def _():
-            for t in range(LAG):
-                for i in range(PIECES):
-                    zx_copy(t, i).start()
-
         @pl.when(s >= LAG)
         def _():
             mlp_chunk(s - LAG)
@@ -400,12 +412,16 @@
 
     def keep_copy(j, place, i):
         rows = piece_rows(i, j * HALF)
-        return pltpu.make_async_copy(stage.at[rows], out_ref.at[piece_rows(i, place * HALF)], keep_sem.at[place // 2, i])
+        return pltpu.make_async_copy(stage.at[rows], out_ref.at[piece_rows(i, place * HALF)], keep_sem.at[lax.div(place, 2), i])
 
     def give_copy(j, i):
         return remote(stage.at[piece_rows(i, j * HALF)], out_ref.at[piece_rows(i, HALF)], out_ss.at[i], out_rs.at[i], mate)
 
-    for j in range(3):
+    for order in range(3):
+        j = jnp.where(chip == 0, (order + 2) % 3, order)
+        place = 2 * (j - core)
+        give = (place < 0) | (place > 2)
+
         def step(i, c):
             zx_copy(j, i).wait_recv()
             rows = sub_rows((3 * chip + j) * HALF, i)
@@ -413,13 +429,13 @@
             final = res[rows, :].astype(F32) + rms(proj, gain4).astype(BF16).astype(F32)
             stage[sub_rows(j * HALF, i), :] = final.astype(BF16)
 
-            @pl.when(core == 0)
+            @pl.when(give)
             def _():
-                (give_copy(j, i) if j == 2 else keep_copy(j, 2 * j, i)).start()
-
-            @pl.when(core == 1)
+                give_copy(j, i).start()
+
+            @pl.when(jnp.logical_not(give))
             def _():
-                (give_copy(j, i) if j == 0 else keep_copy(j, 2 * j - 2, i)).start()
+                keep_copy(j, place, i).start()
             return c
         lax.fori_loop(0, PIECES, step, 0)
 
@@ -438,7 +454,6 @@
 def run_layer(block_rows, looked, tokens, k_pos, inv_freq, w_query, w_key, w_value, w_out, w_gate, w_up, w_down, g1, g2, g3, g4):
     seq, dim = looked.shape
     scale = float(np.sqrt(np.float32(dim)).astype(jnp.bfloat16))
-    vmem = pl.BlockSpec(memory_space=pltpu.VMEM)
     hbm = pl.BlockSpec(memory_space=pl.ANY)
     half_all = pltpu.VMEM((seq // 2, dim), BF16)
     dma = pltpu.SemaphoreType.DMA
@@ -446,9 +461,11 @@
         functools.partial(layer_kernel, block_rows, scale),
         name="layer",
         out_shape=jax.ShapeDtypeStruct((seq // 4, dim), BF16),
-        in_specs=[hbm] + [vmem] * 3 + [hbm] * 7 + [vmem] * 4,
+        in_specs=[hbm] * 15,
         out_specs=hbm,
         scratch_shapes=[
+            pltpu.VMEM(tokens.shape, jnp.int32), pltpu.VMEM(k_pos.shape, jnp.int32), pltpu.VMEM(inv_freq.shape, F32),
+            pltpu.VMEM((dim,), F32), pltpu.VMEM((dim,), F32), pltpu.VMEM((dim,), F32), pltpu.VMEM((dim,), F32),
             pltpu.VMEM((dim, 1024), BF16),
             pltpu.VMEM(w_out.shape, BF16), pltpu.VMEM(w_gate.shape, BF16), pltpu.VMEM(w_up.shape, BF16),
             pltpu.VMEM(w_down.shape, BF16),
@@ -464,7 +481,7 @@
             dma((2,)), dma((2,)), dma, dma,
             dma((N_CHUNK,)), dma((N_CHUNK,)), dma((2,)), dma((2,)), dma, dma((2,)),
             dma((3, PIECES)), dma((3, PIECES)), dma((PIECES,)), dma((PIECES,)), dma((2, PIECES)),
-            dma((PIECES,)), dma((PIECES,)), dma((PIECES,)), dma((PIECES,)), dma((PIECES,)),
+            dma((7,)), dma((PIECES,)), dma((PIECES,)), dma((PIECES,)), dma((PIECES,)), dma((PIECES,)),
         ],
         compiler_params=pltpu.CompilerParams(
             collective_id=0, has_side_effects=True, vmem_limit_bytes=67043328),

time: 129 us -> 128 us (level)
  no operation moved by 1% of the time
where the time goes in v6:
time: 128 us; the launch traced here: 127 us
  Pallas kernels  114 us (89%)
  local copies, waits for them, and re-layouts  12.7 us (10%)
    pallas_call x1, Pallas kernels, run_layer(): pl.pallas_call(functools.partial(layer_kernel, block_rows, scale), name='...  114 us
    gather x1, local copies, waits for them, and re-layouts, device_step(): embed_block.at[lax.rem(tokens[0], block_rows)].get(mode='promise_in_bounds')  10.5 us

profile of v6, /device:TPU:0, one launch (start us, length us, event | category | flops | bytes accessed | tf_op | source)
XLA Modules:
  0.0 127.2 jit_solution(12153942532828542659)
XLA Ops:
  0.0 0.7 fusion
  0.7 10.5 %gather_fusion = bf16[768,2560]{1,0:T(8,128)(2,1)} fusion(bf16[65552,2560]{1,0:T(8,128)(2,1)} %param.17, s32[1024]{0:T(1024)S(1)} %pad_clamp_fusion), kind=kCustom, calls=%fused_computation | custom fusion | bytes 7867392 | tf_op jit(solution)/shard_map/gather | solution.py:497
  11.2 113.8 %layer.1 = bf16[192,2560]{1,0:T(8,128)(2,1)} custom-call(bf16[768,2560]{1,0:T(8,128)(2,1)} %gather_fusion, s32[1,768]{1,0:T(1,128)} %ids_hbm.1, s32[1,768]{1,0:T(1,128)} %kpos_hbm.1, f32[1,128]{1,0:T(1,128)} %constant.6.clone.freq_hbm, bf16[2560,2,256]{2,1,0:T(2,128)(2,1)} %wq_hbm.1, bf16[2560,256]{1,0:T(8,128)(2,1)} %bitcast.8, bf16[2560,256]{1,0:T(8,128)(2,1)} %bitcast.9, ...), custom_call_target="tpu_custom_call" | custom-call | tf_op jit(solution)/shard_map/layer/pallas_call | solution.py:460
  125.0 2.2 %copy.17 = bf16[1,192,2560]{2,1,0:T(8,128)(2,1)} copy(bf16[1,192,2560]{2,1,0:T(8,128)(2,1)} %bitcast.6) | data formatting | bytes 1966080
  (1 shorter events, 0.0 us)

commit v7 on v6

--- a/solution.py
+++ b/solution.py
@@ -116,6 +116,9 @@
             [(wk_hbm, wqkv.at[:, pl.ds(512, 256)]), (wv_hbm, wqkv.at[:, pl.ds(768, 256)]), (wo_hbm, wo), (wg_hbm, wg), (wu_hbm, wu), (wd_hbm, wd)])
     ]
 
+    barrier = pltpu.get_barrier_semaphore()
+    for peer in (far, mate):
+        pl.semaphore_signal(barrier, inc=1, device_id=(dp, peer), device_id_type=MESH)
     for i in range(PIECES):
         stage_copy(i).start()
     own_copy(0).start()
@@ -127,9 +130,6 @@
     ]
     for copy in small:
         copy.start()
-    barrier = pltpu.get_barrier_semaphore()
-    for peer in (mate, far):
-        pl.semaphore_signal(barrier, inc=1, device_id=(dp, peer), device_id_type=MESH)
     pl.semaphore_wait(barrier, 2)
 
     for i in range(PIECES):

time: 128 us -> 128 us (level)
  no operation moved by 1% of the time
where the time goes in v7:
time: 128 us; the launch traced here: 127 us
  Pallas kernels  114 us (89%)
  local copies, waits for them, and re-layouts  12.7 us (10%)
    pallas_call x1, Pallas kernels, run_layer(): pl.pallas_call(functools.partial(layer_kernel, block_rows, scale), name='...  114 us
    gather x1, local copies, waits for them, and re-layouts, device_step(): embed_block.at[lax.rem(tokens[0], block_rows)].get(mode='promise_in_bounds')  10.5 us

profile of v7, /device:TPU:0, one launch (start us, length us, event | category | flops | bytes accessed | tf_op | source)
XLA Modules:
  0.0 127.2 jit_solution(17923537774483749214)
XLA Ops:
  0.0 0.7 fusion
  0.7 10.5 %gather_fusion = bf16[768,2560]{1,0:T(8,128)(2,1)} fusion(bf16[65552,2560]{1,0:T(8,128)(2,1)} %param.17, s32[1024]{0:T(1024)S(1)} %pad_clamp_fusion), kind=kCustom, calls=%fused_computation | custom fusion | bytes 7867392 | tf_op jit(solution)/shard_map/gather | solution.py:497
  11.2 113.8 %layer.1 = bf16[192,2560]{1,0:T(8,128)(2,1)} custom-call(bf16[768,2560]{1,0:T(8,128)(2,1)} %gather_fusion, s32[1,768]{1,0:T(1,128)} %ids_hbm.1, s32[1,768]{1,0:T(1,128)} %kpos_hbm.1, f32[1,128]{1,0:T(1,128)} %constant.6.clone.freq_hbm, bf16[2560,2,256]{2,1,0:T(2,128)(2,1)} %wq_hbm.1, bf16[2560,256]{1,0:T(8,128)(2,1)} %bitcast.8, bf16[2560,256]{1,0:T(8,128)(2,1)} %bitcast.9, ...), custom_call_target="tpu_custom_call" | custom-call | tf_op jit(solution)/shard_map/layer/pallas_call | solution.py:460
  125.0 2.2 %copy.17 = bf16[1,192,2560]{2,1,0:T(8,128)(2,1)} copy(bf16[1,192,2560]{2,1,0:T(8,128)(2,1)} %bitcast.6) | data formatting | bytes 1966080
  (1 shorter events, 0.0 us)
